TPU v7x, 8 devices: a whole 2x2x1 slice. The times are simulated.
8 devices in a mesh: data: 1 (over z), tp: 2 (over y), ep: 4 (over x, core).
Axes of the slice: x: 2, y: 2, z: 1, core: 2. Of those that a mesh axis runs over, the one named last changes fastest.
Arguments:
- tokens: bfloat16 [16384, 2048], P(('data', 'ep', 'tp'))
- expert_ids: int32 [16384, 4], P(('data', 'ep', 'tp'))
- gate_vals: float32 [16384, 4], P(('data', 'ep', 'tp'))
- slot_ids: int32 [16384, 4], P(('data', 'ep', 'tp'))
- send_counts: int32 [8, 60], P(('data', 'ep', 'tp'))
- shared_w1: bfloat16 [2048, 5632], P(None, 'tp')
- shared_w3: bfloat16 [2048, 5632], P(None, 'tp')
- shared_w2: bfloat16 [5632, 2048], P('tp')
- expert_w1: bfloat16 [60, 2048, 1408], P('ep')
- expert_w3: bfloat16 [60, 2048, 1408], P('ep')
- expert_w2: bfloat16 [60, 1408, 2048], P('ep')
Outputs:
- output: bfloat16 [16384, 2048], P(('data', 'ep', 'tp'))
All inputs are finite; a program needn't handle non-finite values.
Results may differ from a plain program's by a relative error of at most 0.00124.
Values are sent between devices in bfloat16 or wider.
A program may use at most 1.25 GiB of HBM per device.

v0:
```python
import jax
import jax.numpy as jnp
from jax import lax
from jax.sharding import PartitionSpec as P

CAP_FACTOR = 4


def capacity_rows(n_tok, top_k, n_exp):
    return min(n_tok, ((CAP_FACTOR * n_tok * top_k // n_exp + 7) // 8) * 8)


def solution(mesh):
    ep_size = mesh.shape["ep"]
    row_spec = P(("data", "ep", "tp"), None)
    expert_spec = P("ep", None, None)

    def layer_body(tokens, expert_ids, gate_vals, slot_ids, send_counts, shared_w1, shared_w3, shared_w2, expert_w1, expert_w3, expert_w2):
        n_tok, d_model = tokens.shape
        top_k = expert_ids.shape[1]
        n_local = expert_w1.shape[0]
        n_exp = n_local * ep_size
        capacity = capacity_rows(n_tok, top_k, n_exp)
        n_rows = n_exp * capacity

        gathered = lax.all_gather(tokens, "tp", axis=0, tiled=True)
        pre_gate = jnp.dot(gathered, shared_w1, preferred_element_type=jnp.float32)
        pre_up = jnp.dot(gathered, shared_w3, preferred_element_type=jnp.float32)
        shared_hidden = (jax.nn.silu(pre_gate) * pre_up).astype(jnp.bfloat16)
        part_sum = jnp.dot(shared_hidden, shared_w2, preferred_element_type=jnp.float32)
        shared_out = lax.psum_scatter(part_sum, "tp", scatter_dimension=0, tiled=True)

        row_limit = jnp.take(send_counts[0], expert_ids, axis=0)
        kept_mask = (slot_ids >= 0) & (slot_ids < row_limit)
        dest_row = jnp.where(kept_mask, expert_ids * capacity + slot_ids, n_rows)
        tok_ids = jnp.broadcast_to(jnp.arange(n_tok, dtype=jnp.int32)[:, None], (n_tok, top_k)).reshape(-1)
        owner_ids = jnp.full((n_rows,), n_tok, jnp.int32).at[dest_row.reshape(-1)].set(tok_ids, mode="drop")
        send_buf = jnp.take(tokens, owner_ids, axis=0, mode="fill", fill_value=0)
        send_buf = send_buf.reshape(ep_size, n_local, capacity, d_model)
        recv_buf = lax.all_to_all(send_buf, "ep", 0, 2, tiled=True)
        recv_buf = recv_buf.reshape(n_local, ep_size * capacity, d_model)

        exp_gate = jnp.einsum("erd,edf->erf", recv_buf, expert_w1, preferred_element_type=jnp.float32)
        exp_up = jnp.einsum("erd,edf->erf", recv_buf, expert_w3, preferred_element_type=jnp.float32)
        exp_hidden = (jax.nn.silu(exp_gate) * exp_up).astype(jnp.bfloat16)
        exp_out = jnp.einsum("erf,efd->erd", exp_hidden, expert_w2, preferred_element_type=jnp.float32).astype(jnp.bfloat16)
        back_buf = lax.all_to_all(exp_out.reshape(1, n_local, ep_size * capacity, d_model), "ep", 2, 0, tiled=True)

        back_rows = back_buf.reshape(n_rows, d_model)
        picked = jnp.take(back_rows, dest_row, axis=0, mode="fill", fill_value=0)
        gate_eff = jnp.where(kept_mask, gate_vals, 0.0)
        routed_sum = jnp.sum(gate_eff[:, :, None] * picked.astype(jnp.float32), axis=1)
        return (tokens.astype(jnp.float32) + shared_out + routed_sum).astype(jnp.bfloat16)

    return jax.shard_map(
        layer_body,
        mesh=mesh,
        in_specs=(row_spec, row_spec, row_spec, row_spec, row_spec, P(None, "tp"), P(None, "tp"), P("tp", None), expert_spec, expert_spec, expert_spec),
        out_specs=row_spec,
        check_vma=False,
    )
```

profile of v0, /device:TPU:0, one launch (start us, length us, event | category | flops | bytes accessed | tf_op | source)
XLA Modules:
  0.0 4800.8 jit_solution(10608698477622066526)
XLA Ops:
  6.5 2.1 fusion.4
  8.6 2.1 fusion.5
  10.7 2.1 fusion.6
  12.8 1.4 fusion.7
  14.2 39.1 compare_and_fusion.1
  53.7 0.7 reshape.68
  54.5 0.6 reshape.160
  55.2 30.5 scatter_custom_fusion
  85.8 0.8 broadcast_in_dim.60
  86.6 248.4 %gather_fusion = bf16[33120,2048]{1,0:T(8,128)(2,1)} fusion(bf16[2048,2048]{1,0:T(8,128)(2,1)} %param.11, s32[33792]{0:T(1024)S(1)} %pad_clamp_fusion), kind=kCustom, calls=%fused_computation | custom fusion | bytes 271451520 | tf_op jit(solution)/shard_map/jit(_take)/gather | solution.py:38
  335.0 86.8 %broadcast_select_fusion = bf16[4,15,552,2048]{3,2,1,0:T(8,128)(2,1)} fusion(bf16[4,15,552,2048]{3,2,1,0:T(8,128)(2,1)} %bitcast.61, pred[4,15,552]{2,1,0:T(8,128)(4,1)S(1)} %copy-done.4), kind=kLoop, calls=%fused_computation.5 | loop fusion | flops 67829760 | bytes 271352160 | tf_op jit(solution)/shard_map/jit(_take)/select_n | solution.py:38
  421.8 25.5 all-to-all-start
  447.6 0.5 all-gather.2.cloned.1.call-update
  448.0 1456.8 %all-to-all-done = bf16[4,15,552,2048]{3,2,1,0:T(8,128)(2,1)} async-done(((bf16[4,15,552,2048]{3,2,1,0:T(8,128)(2,1)}), bf16[4,15,552,2048]{3,2,1,0:T(8,128)(2,1)}, u32[]{:S(2)}, u32[]{:S(2)}) %all-to-all-start) | async-done | bytes 135659552 | tf_op jit(solution)/shard_map/all_to_all | solution.py:40
  1904.9 86.9 %copy.26 = bf16[1,15,4,552,2048]{4,3,2,1,0:T(8,128)(2,1)} copy(bf16[1,15,4,552,2048]{4,3,1,2,0:T(8,128)(2,1)} %bitcast.63) | data formatting | bytes 271319040 | tf_op jit(solution)/shard_map/all_to_all | solution.py:40
  1991.8 223.9 %fusion.10 = f32[15,2208,1408]{2,1,0:T(8,128)} fusion(bf16[15,2208,2048]{2,1,0:T(8,128)(2,1)} %bitcast.64, bf16[15,2048,1408]{2,1,0:T(8,128)(2,1)} %param.19), kind=kOutput, calls=%fused_computation.31 | convolution fusion | flops 191008604160 | bytes 408698880 | tf_op jit(solution)/shard_map/erd,edf->erf/dot_general | solution.py:43
  2215.7 234.6 %multiply_convert_fusion.clone.4 = bf16[15,2208,1408]{2,1,0:T(8,128)(2,1)} fusion(f32[15,2208,1408]{2,1,0:T(8,128)} %fusion.10, bf16[15,2208,2048]{2,1,0:T(8,128)(2,1)} %bitcast.64, bf16[15,2048,1408]{2,1,0:T(8,128)(2,1)} %param.20), kind=kOutput, calls=%fused_computation.3.clone.clone.clone.1 | convolution fusion | flops 191288393728 | bytes 501964800 | tf_op jit(solution)/shard_map/erd,edf->erf/dot_general | solution.py:44
  2450.3 222.6 %convert_bitcast_fusion = bf16[1,15,2208,2048]{3,2,1,0:T(8,128)(2,1)} fusion(bf16[15,1408,2048]{2,1,0:T(8,128)(2,1)} %param.21, bf16[15,2208,1408]{2,1,0:T(8,128)(2,1)} %multiply_convert_fusion.clone.4), kind=kOutput, calls=%fused_computation.4 | convolution fusion | flops 191076433920 | bytes 315432960 | tf_op jit(solution)/shard_map/erf,efd->erd/dot_general | solution.py:46
  2672.9 115.4 %copy.27 = bf16[1,15,2208,2048]{3,1,0,2:T(8,128)(2,1)} copy(bf16[1,15,2208,2048]{3,2,1,0:T(8,128)(2,1)} %convert_bitcast_fusion) | data formatting | bytes 271319040 | tf_op jit(solution)/shard_map/reshape | solution.py:47
  2788.3 26.4 all-to-all-start.1
  2814.8 57.6 %fusion.8 = f32[4096,2816]{1,0:T(8,128)} fusion(bf16[4096,2048]{1,0:T(8,128)(2,1)} %all-gather.2.cloned.1.call-done, bf16[2048,2816]{1,0:T(8,128)(2,1)} %param.16), kind=kOutput, calls=%fused_computation.29 | convolution fusion | flops 47244640256 | bytes 74448896 | tf_op jit(solution)/shard_map/dot_general | solution.py:27
  2872.4 59.8 %multiply_convert_fusion.1 = bf16[4096,2816]{1,0:T(8,128)(2,1)} fusion(f32[4096,2816]{1,0:T(8,128)} %fusion.8, bf16[4096,2048]{1,0:T(8,128)(2,1)} %all-gather.2.cloned.1.call-done, bf16[2048,2816]{1,0:T(8,128)(2,1)} %param.17), kind=kOutput, calls=%fused_computation.7 | convolution fusion | flops 47313846272 | bytes 97517568 | tf_op jit(solution)/shard_map/dot_general | solution.py:28
  2932.2 56.8 %fusion.9 = f32[4096,2048]{1,0:T(8,128)} fusion(bf16[4096,2816]{1,0:T(8,128)(2,1)} %multiply_convert_fusion.1, bf16[2816,2048]{1,0:T(8,128)(2,1)} %param.18), kind=kOutput, calls=%fused_computation.30 | convolution fusion | flops 47244640256 | bytes 68157440 | tf_op jit(solution)/shard_map/dot_general | solution.py:30
  2989.4 0.6 reshape.150
  2990.1 1.3 copy.23
  2991.4 1.1 copy.24
  2992.5 1375.6 %all-to-all-done.1 = bf16[1,15,2208,2048]{3,1,0,2:T(8,128)(2,1)} async-done(((bf16[1,15,2208,2048]{3,1,0,2:T(8,128)(2,1)}), bf16[1,15,2208,2048]{3,1,0,2:T(8,128)(2,1)}, u32[]{:S(2)}, u32[]{:S(2)}) %all-to-all-start.1) | async-done | bytes 135659552 | tf_op jit(solution)/shard_map/all_to_all | solution.py:47
  4368.1 91.1 %copy.28 = bf16[1,15,4,552,2048]{4,3,1,2,0:T(8,128)(2,1)} copy(bf16[1,15,4,552,2048]{4,1,3,2,0:T(8,128)(2,1)} %bitcast.66) | data formatting | bytes 271319040 | tf_op jit(solution)/shard_map/all_to_all | solution.py:47
  4459.2 190.9 %gather_fusion.1 = bf16[8192,2048]{1,0:T(8,128)(2,1)} fusion(bf16[33120,2048]{1,0:T(8,128)(2,1)} %bitcast.68, s32[8192]{0:T(1024)S(1)} %broadcast_clamp_fusion), kind=kCustom, calls=%fused_computation.1 | custom fusion | bytes 67141632 | tf_op jit(solution)/shard_map/jit(_take)/gather | solution.py:50
  4650.1 48.5 %reshape.149 = bf16[2048,4,2048]{2,1,0:T(4,128)(2,1)} reshape(bf16[8192,2048]{1,0:T(8,128)(2,1)} %gather_fusion.1) | data formatting | bytes 67108864 | tf_op jit(solution)/shard_map/jit(_take)/gather | solution.py:50
  4698.6 77.0 %multiply_reduce_fusion = f32[2048,2048]{1,0:T(8,128)} fusion(bf16[2048,4,2048]{2,1,0:T(4,128)(2,1)} %reshape.149, f32[2048,4]{1,0:T(8,128)S(1)} %copy-done, pred[2048,4]{1,0:T(8,128)(4,1)S(1)} %copy-done.1), kind=kLoop, calls=%fused_computation.6 | loop fusion | flops 62914560 | bytes 50372608 | tf_op jit(solution)/shard_map/reduce_sum | solution.py:52
  4775.6 18.0 add_convert_fusion
  (31 shorter events, 1.3 us)
Async XLA Ops:
  53.3 281.7 %copy-start.2 = (s32[2048,4]{0,1:T(4,128)}, s32[2048,4]{0,1:T(4,128)S(1)}, u32[]{:S(2)}) copy-start(s32[2048,4]{0,1:T(4,128)S(1)} %get-tuple-element.6) | copy-start | bytes 98308
  86.6 248.4 %copy-start.4 = (pred[4,15,552]{2,1,0:T(8,128)(4,1)S(1)}, pred[4,15,552]{2,1,0:T(8,128)(4,1)}, u32[]{:S(2)}) copy-start(pred[4,15,552]{2,1,0:T(8,128)(4,1)} %broadcast_in_dim.60) | copy-start | bytes 99364
  421.8 1483.0 %all-to-all-start = ((bf16[4,15,552,2048]{3,2,1,0:T(8,128)(2,1)}), bf16[4,15,552,2048]{3,2,1,0:T(8,128)(2,1)}, u32[]{:S(2)}, u32[]{:S(2)}) async-start(bf16[4,15,552,2048]{3,2,1,0:T(8,128)(2,1)} %broadcast_select_fusion), calls=%async_computation.1 | async-start | bytes 271319040 | tf_op jit(solution)/shard_map/all_to_all | solution.py:40
  447.3 2367.5 %all-gather.2.cloned.1.call-start = ((), (), s32[]{:S(2)}) async-start(), calls=%async_computation.3 | async-start | bytes 25165824 | tf_op jit(solution)/shard_map/all_gather | solution.py:26
  2788.3 1579.8 %all-to-all-start.1 = ((bf16[1,15,2208,2048]{3,1,0,2:T(8,128)(2,1)}), bf16[1,15,2208,2048]{3,1,0,2:T(8,128)(2,1)}, u32[]{:S(2)}, u32[]{:S(2)}) async-start(bf16[1,15,2208,2048]{3,1,0,2:T(8,128)(2,1)} %copy.27), calls=%async_computation.2 | async-start | bytes 289406976 | tf_op jit(solution)/shard_map/all_to_all | solution.py:47
  2814.7 1960.9 %reduce-scatter.2.cloned.1.call-start = ((), (), s32[]{:S(2)}) async-start(), calls=%async_computation.4 | async-start | bytes 50331648 | tf_op jit(solution)/shard_map/reduce_scatter | solution.py:31
  2932.2 56.8 %copy-start.3 = (s32[2048,4]{0,1:T(4,128)S(1)}, s32[2048,4]{0,1:T(4,128)}, u32[]{:S(2)}) copy-start(s32[2048,4]{0,1:T(4,128)} %copy-done.2) | copy-start | bytes 98308
  2932.2 57.9 %copy-start.6 = (pred[2048,4]{0,1:T(4,128)(4,1)S(1)}, pred[2048,4]{0,1:T(4,128)(4,1)}, u32[]{:S(2)}) copy-start(pred[2048,4]{0,1:T(4,128)(4,1)} %get-tuple-element.7) | copy-start | bytes 24580
  2932.2 57.9 %copy-start.7 = (f32[2048,4]{0,1:T(4,128)S(1)}, f32[2048,4]{0,1:T(4,128)}, u32[]{:S(2)}) copy-start(f32[2048,4]{0,1:T(4,128)} %param.13) | copy-start | bytes 98308
  2932.2 59.2 %copy-start.5 = (pred[2048,4]{0,1:T(4,128)(4,1)S(1)}, pred[2048,4]{0,1:T(4,128)(4,1)}, u32[]{:S(2)}) copy-start(pred[2048,4]{0,1:T(4,128)(4,1)} %get-tuple-element.5) | copy-start | bytes 24580
  4650.1 48.5 %copy-start = (f32[2048,4]{1,0:T(8,128)S(1)}, f32[2048,4]{1,0:T(8,128)}, u32[]{:S(2)}) copy-start(f32[2048,4]{1,0:T(8,128)} %copy.23) | copy-start | bytes 98308
  4650.1 48.5 %copy-start.1 = (pred[2048,4]{1,0:T(8,128)(4,1)S(1)}, pred[2048,4]{1,0:T(8,128)(4,1)}, u32[]{:S(2)}) copy-start(pred[2048,4]{1,0:T(8,128)(4,1)} %copy.24) | copy-start | bytes 24580
Sparse Core Ops, SparseCore 0:
  449.6 199.9 all-gather.1
  2989.1 368.2 reduce-scatter.1
where the time goes:
time: 4810 us; the launch traced here: 4800 us
  waiting for transfers between devices  2830 us (59%)
  matrix products  855 us (18%)
  local copies, waits for them, and re-layouts  825 us (17%)
  other arithmetic  221 us (5%)
  starting transfers between devices  52.1 us (1%)
    all_to_all x1, waiting for transfers between devices, layer_body(): recv_buf = lax.all_to_all(send_buf, 'ep', 0, 2, tiled=True)  1460 us
    all_to_all x1, waiting for transfers between devices, layer_body(): lax.all_to_all(exp_out.reshape(1, n_local, ep_size * capacity, d_model),...  1380 us
    gather x1, local copies, waits for them, and re-layouts, layer_body(): send_buf = jnp.take(tokens, owner_ids, axis=0, mode='fill', fill_value=0)  248 us
    gather x2, local copies, waits for them, and re-layouts, layer_body(): picked = jnp.take(back_rows, dest_row, axis=0, mode='fill', fill_value=0)  239 us
    dot_general x1, matrix products, layer_body(): jnp.einsum('erd,edf->erf', recv_buf, expert_w3, preferred_element_type=jn...  235 us
    dot_general x1, matrix products, layer_body(): jnp.einsum('erd,edf->erf', recv_buf, expert_w1, preferred_element_type=jn...  224 us
    dot_general x1, matrix products, layer_body(): jnp.einsum('erf,efd->erd', exp_hidden, expert_w2, preferred_element_type=...  223 us
    reshape x1, local copies, waits for them, and re-layouts, layer_body(): exp_out.reshape(1, n_local, ep_size * capacity, d_model)  115 us
  transfers between devices with their start and end apart: 4, of which 2 were waited for; matrix products, arithmetic and copies ran while one was open for 31% of the time, Pallas kernels for 0%

commit v1 on v0

v1 whole, which is shorter than its diff:
```python
import functools

import jax
import jax.numpy as jnp
from jax import lax
from jax.experimental import pallas as pl
from jax.experimental.pallas import tpu as pltpu
from jax.sharding import PartitionSpec as P


CAP_FACTOR = 4
TILE = 256
UNROLL = 8
PAIR = 2
LANES = 128


def capacity_rows(n_tok, top_k, n_exp):
    return min(n_tok, ((CAP_FACTOR * n_tok * top_k // n_exp + 7) // 8) * 8)


def token_of(copy_id, top_k):
    return lax.div(copy_id, top_k) if top_k & (top_k - 1) else lax.shift_right_logical(copy_id, top_k.bit_length() - 1)


def segment(offs, expert, start, q):
    base = offs[expert * (PAIR + 1) + q]
    lo = jnp.maximum(base, start)
    hi = jnp.minimum(offs[expert * (PAIR + 1) + q + 1], start + TILE)
    return lo - start, jnp.maximum(hi - lo, 0), lo - base


def up_kernel(n_tok, top_k, n_local, table_cols, tile_exp, tile_row, offs, owner, x0, x1, w1_ref, w3_ref, u_ref, tok_vmem, rows_vmem, sems):
    step = pl.program_id(0)

    @pl.when(step == 0)
    def _():
        copies = [pltpu.make_async_copy(src, tok_vmem.at[pl.ds(q * n_tok, n_tok)], sems.at[q]) for q, src in enumerate((x0, x1))]
        for copy in copies:
            copy.start()
        for copy in copies:
            copy.wait()

    @pl.when(step < tile_row[pl.num_programs(0)])
    def _():
        expert, start = tile_exp[step], tile_row[step]
        for q in range(PAIR):
            dst, count, slot = segment(offs, expert, start, q)
            src = (q * n_local + expert) * table_cols + slot

            def gather(g, carry):
                rows = [tok_vmem[token_of(owner[src + g * UNROLL + j], top_k)] for j in range(UNROLL)]
                for j in range(UNROLL):
                    rows_vmem[dst + g * UNROLL + j] = rows[j]
                return carry

            lax.fori_loop(0, lax.div(count, UNROLL), gather, 0)

        rows = rows_vmem[...].reshape(TILE, -1)
        pre_gate = jnp.dot(rows, w1_ref[0], preferred_element_type=jnp.float32)
        pre_up = jnp.dot(rows, w3_ref[0], preferred_element_type=jnp.float32)
        u_ref[...] = (jax.nn.silu(pre_gate) * pre_up).astype(jnp.bfloat16)


def down_kernel(n_tok, top_k, n_local, table_cols, tile_exp, tile_row, offs, owner, gates, u_ref, w2_ref, *refs):
    *outs, acc, tile_vmem, sems = refs
    step = pl.program_id(0)
    cols = w2_ref.shape[2] // LANES

    @pl.when(step == 0)
    def _():
        def clear(g, carry):
            acc[pl.ds(g * 8, 8)] = jnp.zeros((8, cols, LANES), jnp.float32)
            return carry

        lax.fori_loop(0, PAIR * n_tok // 8, clear, 0)

    @pl.when(step < tile_row[pl.num_programs(0)])
    def _():
        out = jnp.dot(u_ref[...], w2_ref[0], preferred_element_type=jnp.float32).astype(jnp.bfloat16).astype(jnp.float32)
        for b in range(TILE // 8):
            for c in range(cols):
                tile_vmem[pl.ds(b * 8 * cols + c, 8, stride=cols), :] = out[b * 8 : (b + 1) * 8, c * LANES : (c + 1) * LANES]

        expert, start = tile_exp[step], tile_row[step]
        for q in range(PAIR):
            dst, count, slot = segment(offs, expert, start, q)
            src = (q * n_local + expert) * table_cols + slot

            def scatter(g, carry):
                copy_ids = [owner[src + g * UNROLL + j] for j in range(UNROLL)]
                toks = [token_of(copy_id, top_k) for copy_id in copy_ids]
                firsts = [pl.multiple_of((dst + g * UNROLL + j) * cols, cols) for j in range(UNROLL)]
                vals = [tile_vmem[pl.ds(firsts[j], cols), :] * gates[copy_ids[j]] for j in range(UNROLL)]
                olds = [acc[t] for t in toks]
                for j in range(UNROLL):
                    acc[toks[j]] = olds[j] + vals[j]
                return carry

            lax.fori_loop(0, lax.div(count, UNROLL), scatter, 0)

    @pl.when(step == pl.num_programs(0) - 1)
    def _():
        rows = PAIR * n_tok // len(outs)
        copies = [pltpu.make_async_copy(acc.at[pl.ds(i * rows, rows)], dst, sems.at[i]) for i, dst in enumerate(outs)]
        for copy in copies:
            copy.start()
        for copy in copies:
            copy.wait()


def solution(mesh):
    ep_size = mesh.shape["ep"]
    row_spec = P(("data", "ep", "tp"), None)
    expert_spec = P("ep", None, None)
    core_swap = [(r, r ^ 1) for r in range(ep_size)]
    chip_swap = [(r, r ^ 2) for r in range(ep_size)]

    def layer_body(tokens, expert_ids, gate_vals, slot_ids, send_counts, shared_w1, shared_w3, shared_w2, expert_w1, expert_w3, expert_w2):
        n_tok, d_model = tokens.shape
        top_k = expert_ids.shape[1]
        n_local, _, d_ff = expert_w1.shape
        n_exp = n_local * ep_size
        capacity = capacity_rows(n_tok, top_k, n_exp)
        table_cols = capacity + UNROLL
        max_tiles = n_local * PAIR * (capacity + UNROLL - 1) // TILE + n_local
        rank = lax.axis_index("ep")

        toks3 = tokens.reshape(n_tok, d_model // LANES, LANES)
        x_chip = lax.ppermute(toks3, "ep", chip_swap)
        x_core = lax.ppermute(toks3, "ep", core_swap)
        x_diag = lax.ppermute(x_chip, "ep", core_swap)
        peer_tokens = lax.ppermute(tokens, "tp", [(0, 1), (1, 0)])

        slots = jnp.where((slot_ids >= 0) & (slot_ids < capacity), slot_ids, table_cols)
        copy_ids = jnp.arange(n_tok * top_k, dtype=jnp.int32)
        dest = jnp.where(slots < capacity, expert_ids * table_cols + slots, n_exp * table_cols).reshape(-1)
        owner = jnp.zeros((n_exp * table_cols,), jnp.int32).at[dest].set(copy_ids, mode="drop").reshape(n_exp, table_cols)
        owner = jnp.concatenate([owner[:, :-1], send_counts[0][:, None]], axis=1)
        order = rank ^ jnp.arange(ep_size, dtype=jnp.int32)
        owner = lax.all_to_all(owner.reshape(ep_size, n_local, table_cols), "ep", 0, 0, tiled=True)
        owner = jnp.take(owner, order, axis=0)
        gates = lax.all_gather(gate_vals.reshape(-1), "ep", axis=0)
        gates = jnp.take(gates, order, axis=0)

        counts = jnp.minimum(owner[:, :, -1], capacity)

        any_spec = pl.BlockSpec(memory_space=pl.ANY)
        avg_rows = PAIR * n_tok * top_k // 2

        def plan(first):
            cnt = counts[first : first + PAIR]
            padded = (cnt + UNROLL - 1) // UNROLL * UNROLL
            offs = jnp.concatenate([jnp.zeros((1, n_local), jnp.int32), jnp.cumsum(padded, axis=0, dtype=jnp.int32)], axis=0)
            tiles = (offs[-1] + TILE - 1) // TILE
            ends = jnp.cumsum(tiles, dtype=jnp.int32)
            last = jnp.maximum(ends[-1], 1) - 1
            ids = jnp.minimum(jnp.arange(max_tiles, dtype=jnp.int32), last)
            past = ids[:, None] >= ends[None, :]
            tile_exp = jnp.minimum(jnp.sum(past, axis=1, dtype=jnp.int32), n_local - 1)
            tile_row = jnp.append((ids - jnp.sum(jnp.where(past, tiles[None, :], 0), axis=1, dtype=jnp.int32)) * TILE, last + 1)
            col = jnp.arange(table_cols, dtype=jnp.int32)
            base = jnp.arange(PAIR, dtype=jnp.int32)[:, None, None] * (n_tok * top_k)
            spare = PAIR * n_tok * top_k + (col % UNROLL) * top_k
            rows = jnp.where(col < cnt[:, :, None], owner[first : first + PAIR] + base, spare).reshape(-1)
            gate = jnp.append(gates[first : first + PAIR].reshape(-1), jnp.zeros((UNROLL * top_k,), jnp.float32))
            return tile_exp, tile_row, offs.T.reshape(-1), rows, gate

        def experts(planned, rows0, rows1, n_out):
            tile_exp, tile_row, offs, rows, gate = planned
            hidden = pl.pallas_call(
                functools.partial(up_kernel, n_tok, top_k, n_local, table_cols),
                grid_spec=pltpu.PrefetchScalarGridSpec(
                    num_scalar_prefetch=4,
                    grid=(max_tiles,),
                    in_specs=[any_spec] * PAIR + [pl.BlockSpec((1, d_model, d_ff), lambda i, te, tr, of, ow: (te[i], 0, 0))] * 2,
                    out_specs=pl.BlockSpec((TILE, d_ff), lambda i, te, tr, of, ow: (jnp.minimum(i, tr[max_tiles] - 1), 0)),
                    scratch_shapes=[
                        pltpu.VMEM((PAIR * n_tok + UNROLL, d_model // LANES, LANES), jnp.bfloat16),
                        pltpu.VMEM((TILE, d_model // LANES, LANES), jnp.bfloat16),
                        pltpu.SemaphoreType.DMA((PAIR,)),
                    ],
                ),
                out_shape=jax.ShapeDtypeStruct((max_tiles * TILE, d_ff), jnp.bfloat16),
                compiler_params=pltpu.CompilerParams(vmem_limit_bytes=60 * 2**20, dimension_semantics=("arbitrary",)),
                cost_estimate=pl.CostEstimate(flops=4 * avg_rows * d_model * d_ff, bytes_accessed=4 * n_local * d_model * d_ff, transcendentals=0),
                name="expert_up",
            )(tile_exp, tile_row, offs, rows, rows0, rows1, expert_w1, expert_w3)
            return pl.pallas_call(
                functools.partial(down_kernel, n_tok, top_k, n_local, table_cols),
                grid_spec=pltpu.PrefetchScalarGridSpec(
                    num_scalar_prefetch=5,
                    grid=(max_tiles,),
                    in_specs=[
                        pl.BlockSpec((TILE, d_ff), lambda i, te, tr, of, ow, ga: (jnp.minimum(i, tr[max_tiles] - 1), 0)),
                        pl.BlockSpec((1, d_ff, d_model), lambda i, te, tr, of, ow, ga: (te[i], 0, 0)),
                    ],
                    out_specs=[any_spec] * n_out,
                    scratch_shapes=[
                        pltpu.VMEM((PAIR * n_tok + UNROLL, d_model // LANES, LANES), jnp.float32),
                        pltpu.VMEM((TILE * d_model // LANES, LANES), jnp.float32),
                        pltpu.SemaphoreType.DMA((n_out,)),
                    ],
                ),
                out_shape=[jax.ShapeDtypeStruct((PAIR * n_tok // n_out, d_model // LANES, LANES), jnp.float32)] * n_out,
                compiler_params=pltpu.CompilerParams(vmem_limit_bytes=60 * 2**20, dimension_semantics=("arbitrary",)),
                cost_estimate=pl.CostEstimate(flops=2 * avg_rows * d_model * d_ff, bytes_accessed=2 * n_local * d_model * d_ff, transcendentals=0),
                name="expert_down",
            )(tile_exp, tile_row, offs, rows, gate, hidden, expert_w2)

        def shared_part(rows):
            pre_gate = jnp.dot(rows, shared_w1, preferred_element_type=jnp.float32)
            pre_up = jnp.dot(rows, shared_w3, preferred_element_type=jnp.float32)
            shared_hidden = (jax.nn.silu(pre_gate) * pre_up).astype(jnp.bfloat16)
            return jnp.dot(shared_hidden, shared_w2, preferred_element_type=jnp.float32)

        far_plan, near_plan = plan(PAIR), plan(0)
        own_part = shared_part(tokens)
        tile_exp, own_part = lax.optimization_barrier((far_plan[0], own_part))
        far_sums = experts((tile_exp, *far_plan[1:]), x_chip, x_diag, 4)
        peer_tokens, *far_sums = lax.optimization_barrier((peer_tokens, *far_sums))
        peer_rows = jnp.split(peer_tokens, 2)
        swapped = [lax.ppermute(part, "ep", core_swap) for part in far_sums[2:]]
        peer_0 = shared_part(peer_rows[0])
        swapped[0], peer_0 = lax.optimization_barrier((swapped[0], peer_0))
        chip_sums = [mine + theirs for mine, theirs in zip(far_sums[:2], swapped)]
        rows_1, *chip_sums = lax.optimization_barrier((peer_rows[1], *chip_sums))
        back = [lax.ppermute(part, "ep", chip_swap) for part in chip_sums]
        peer_1 = shared_part(rows_1)
        tile_exp, peer_1 = lax.optimization_barrier((near_plan[0], peer_1))
        peer_back = [lax.ppermute(part, "tp", [(0, 1), (1, 0)]) for part in (peer_0, peer_1)]
        own, core = experts((tile_exp, *near_plan[1:]), toks3, x_core, 2)
        near = (own + lax.ppermute(core, "ep", core_swap)).reshape(n_tok, d_model)
        kept = tokens.astype(jnp.float32) + own_part + near
        routed = jnp.concatenate([part.reshape(-1, d_model) for part in back])
        return (kept + jnp.concatenate(peer_back) + routed).astype(jnp.bfloat16)

    return jax.shard_map(
        layer_body,
        mesh=mesh,
        in_specs=(row_spec, row_spec, row_spec, row_spec, row_spec, P(None, "tp"), P(None, "tp"), P("tp", None), expert_spec, expert_spec, expert_spec),
        out_specs=row_spec,
        check_vma=False,
    )
```

time: 4810 us -> 1350 us (0.28)
  waiting for transfers between devices: 2830 us -> 352 us
  local copies, waits for them, and re-layouts: 825 us -> 74.9 us
  matrix products: 855 us -> 206 us
  Pallas kernels: 0 us -> 297 us
  starting transfers between devices: 52.1 us -> 232 us
  other arithmetic: 221 us -> 67.2 us
  blocking collectives: 0 us -> 115 us
    all_to_all x2 -> x1, waiting for transfers between devices: 2830 us -> 0.01 us  [layer_body(): lax.all_to_all(owner.reshape(ep_size, n_local, table_cols), 'ep', 0, 0, t...]
    dot_general x6 -> x7, matrix products: 855 us -> 206 us  [the longest x3 104 us: shared_part(): return jnp.dot(shared_hidden, shared_w2, preferred_element_type=jnp.float32)]
    gather x7 -> x2, local copies, waits for them, and re-layouts: 495 us -> 2.2 us  [the longest x1 1.59 us: layer_body(): owner = jnp.take(owner, order, axis=0)]
    ppermute x0 -> x11, waiting for transfers between devices: none -> 352 us  [the longest x2 352 us: layer_body(): back = [lax.ppermute(part, 'ep', chip_swap) for part in chip_sums]]
    pallas_call x0 -> x4, Pallas kernels: none -> 297 us  [the longest x2 166 us: experts(): pl.pallas_call(functools.partial(up_kernel, n_tok, top_k, n_local, table_...]
    ppermute x0 -> x11, starting transfers between devices: none -> 228 us  [the longest x1 84.5 us: layer_body(): near = (own + lax.ppermute(core, 'ep', core_swap)).reshape(n_tok, d_model)]
    all_to_all x2 -> x0, local copies, waits for them, and re-layouts: 178 us -> none  [the longest x1 91.1 us: layer_body(): lax.all_to_all(exp_out.reshape(1, n_local, ep_size * capacity, d_model),...]
    all_gather x0 -> x1, blocking collectives: none -> 115 us  [layer_body(): gates = lax.all_gather(gate_vals.reshape(-1), 'ep', axis=0)]
  transfers between devices with their start and end apart: 4 -> 12, of which waited for: 2 -> 2; matrix products, arithmetic and copies ran while one was open for 31% -> 23% of each run, Pallas kernels for 0% -> 11%
where the time goes in v1:
time: 1350 us
  waiting for transfers between devices  352 us (26%)
  Pallas kernels  297 us (22%)
  starting transfers between devices  232 us (17%)
  matrix products  206 us (15%)
  blocking collectives  115 us (9%)
  local copies, waits for them, and re-layouts  74.9 us (6%)
  other arithmetic  67.2 us (5%)
    ppermute x2, waiting for transfers between devices, layer_body(): back = [lax.ppermute(part, 'ep', chip_swap) for part in chip_sums]  352 us
    pallas_call x2, Pallas kernels, experts(): pl.pallas_call(functools.partial(up_kernel, n_tok, top_k, n_local, table_...  166 us
    pallas_call x2, Pallas kernels, experts(): pl.pallas_call(functools.partial(down_kernel, n_tok, top_k, n_local, tabl...  131 us
    all_gather x1, blocking collectives, layer_body(): gates = lax.all_gather(gate_vals.reshape(-1), 'ep', axis=0)  115 us
    dot_general x3, matrix products, shared_part(): return jnp.dot(shared_hidden, shared_w2, preferred_element_type=jnp.float32)  104 us
    ppermute x1, starting transfers between devices, layer_body(): near = (own + lax.ppermute(core, 'ep', core_swap)).reshape(n_tok, d_model)  84.5 us
    ppermute x2, starting transfers between devices, layer_body(): swapped = [lax.ppermute(part, 'ep', core_swap) for part in far_sums[2:]]  83.9 us
    dot_general x3, matrix products, shared_part(): pre_gate = jnp.dot(rows, shared_w1, preferred_element_type=jnp.float32)  68.3 us
  transfers between devices with their start and end apart: 12, of which 2 were waited for; matrix products, arithmetic and copies ran while one was open for 23% of the time, Pallas kernels for 11%

profile of v1, /device:TPU:0, one launch (start us, length us, event | category | flops | bytes accessed | tf_op | source)
XLA Modules:
  0.0 1345.5 jit_solution(3663591468112481245)
XLA Ops:
  0.0 10.0 copy.40
  10.0 0.8 collective-permute-start.5
  10.8 2.5 collective-permute-start.1
  13.3 1.5 collective-permute-start
  17.4 30.5 %scatter_custom_fusion = s32[33600]{0:T(1024)S(1)} fusion(s32[8192]{0:T(1024)S(1)} %bitcast.107, s32[8192]{0:T(1024)S(1)} %iota.38, s32[]{:T(128)} %constant.132.clone.1), kind=kCustom, calls=%fused_computation.27 | custom fusion | bytes 134404 | tf_op jit(solution)/shard_map/scatter | solution.py:138
  48.8 4.0 all-to-all-start
  52.8 31.9 %fusion.30 = f32[2048,2816]{1,0:T(8,128)} fusion(bf16[2048,2048]{1,0:T(8,128)(2,1)} %param.11, bf16[2048,2816]{1,0:T(8,128)(2,1)} %param.16), kind=kOutput, calls=%fused_computation.101 | convolution fusion | flops 23622320128 | bytes 42991616 | tf_op jit(solution)/shard_map/dot_general | solution.py:212
  85.8 114.6 %all-gather = f32[4,1,8192]{2,1,0:T(1,128)S(1)} all-gather(f32[1,1,8192]{2,1,0:T(1,128)S(1)} %reshape.289), channel_id=1, replica_groups=mesh['data'=1,'tp'=2,'ep'=4] {'ep'}, dimensions={0}, use_global_device_ids=true | all-gather | bytes 163840 | tf_op jit(solution)/shard_map/all_gather | solution.py:143
  201.3 34.3 %multiply_convert_fusion.clone.4 = bf16[2048,2816]{1,0:T(8,128)(2,1)} fusion(f32[2048,2816]{1,0:T(8,128)} %fusion.30, bf16[2048,2048]{1,0:T(8,128)(2,1)} %param.11, bf16[2048,2816]{1,0:T(8,128)(2,1)} %param.17), kind=kOutput, calls=%fused_computation.3.clone.clone.clone.1 | convolution fusion | flops 23656923136 | bytes 54525952 | tf_op jit(solution)/shard_map/dot_general | solution.py:213
  237.0 31.9 %fusion.3 = f32[2048,2048]{1,0:T(8,128)} fusion(bf16[2816,2048]{1,0:T(8,128)(2,1)} %param.18, bf16[2048,2816]{1,0:T(8,128)(2,1)} %multiply_convert_fusion.clone.4), kind=kOutput, calls=%fused_computation.10 | convolution fusion | flops 23622320128 | bytes 39845888 | tf_op jit(solution)/shard_map/dot_general | solution.py:215
  268.9 1.6 gather_fusion
  279.6 83.2 %expert_up.2.u_ref = bf16[20480,1408]{1,0:T(8,128)(2,1)} custom-call(s32[80]{0:T(128)} %broadcast_minimum_fusion.1.tile_exp, s32[81]{0:T(128)} %pad_add_fusion.1.tile_row, s32[45]{0:T(128)} %reshape.254.offs, s32[16800]{0:T(1024)} %reshape.255.owner, bf16[2048,16,128]{2,1,0:T(8,128)(2,1)} %collective-permute-done.1.x0, ...), custom_call_target="tpu_custom_call" | custom-call | flops 94489280512 | bytes 173015040 | tf_op jit(solution)/shard_map/expert_up/pallas_call | solution.py:171
  362.8 65.7 %expert_down.2 = (f32[1024,16,128]{2,1,0:T(8,128)}, f32[1024,16,128]{2,1,0:T(8,128)}, f32[1024,16,128]{2,1,0:T(8,128)}, f32[1024,16,128]{2,1,0:T(8,128)}) custom-call(s32[80]{0:T(128)} %broadcast_minimum_fusion.1.tile_exp, s32[81]{0:T(128)} %pad_add_fusion.1.tile_row, s32[45]{0:T(128)} %reshape.254.offs, s32[16800]{0:T(1024)} %reshape.255.owner, ...), custom_call_target="tpu_custom_call" | custom-call | flops 47244640256 | bytes 86507520 | tf_op jit(solution)/shard_map/expert_down/pallas_call | solution.py:189
  428.6 4.8 split.6
  433.4 83.9 %collective-permute-start.3 = (f32[1024,16,128]{2,1,0:T(8,128)}, f32[1024,16,128]{2,1,0:T(8,128)}, u32[]{:S(2)}, u32[]{:S(2)}) collective-permute-start(f32[1024,16,128]{2,1,0:T(8,128)} %get-tuple-element.33), channel_id=1, source_target_pairs={{0,1},{1,0},{2,3},{3,2},{4,5},{5,4},{6,7},{7,6}} | collective-permute-start | bytes 25165832 | tf_op jit(solution)/shard_map/ppermute | solution.py:223
  517.3 18.7 %fusion.5 = f32[1024,2816]{1,0:T(8,128)} fusion(bf16[2048,2816]{1,0:T(8,128)(2,1)} %param.16, bf16[2048,2048]{1,0:T(8,128)(2,1)} %collective-permute-done), kind=kOutput, calls=%fused_computation.14 | convolution fusion | flops 11811160064 | bytes 27262976 | tf_op jit(solution)/shard_map/dot_general | solution.py:212
  536.0 35.8 %fusion.8 = f32[1024,2048]{1,0:T(8,128)} fusion(bf16[2816,2048]{1,0:T(8,128)(2,1)} %param.18, f32[1024,2816]{1,0:T(8,128)} %fusion.5, bf16[2048,2816]{1,0:T(8,128)(2,1)} %param.17, bf16[2048,2048]{1,0:T(8,128)(2,1)} %collective-permute-done), kind=kOutput, calls=%fused_computation.16 | convolution fusion | flops 23639621632 | bytes 47185920 | tf_op jit(solution)/shard_map/dot_general | solution.py:215
  571.8 10.1 add.189
  581.9 10.3 add.190
  592.2 17.7 %fusion.31 = f32[1024,2816]{1,0:T(8,128)} fusion(bf16[1024,2048]{1,0:T(8,128)(2,1)S(1)} %copy-done, bf16[2048,2816]{1,0:T(8,128)(2,1)} %param.16), kind=kOutput, calls=%fused_computation.102 | convolution fusion | flops 11811160064 | bytes 27262976 | tf_op jit(solution)/shard_map/dot_general | solution.py:212
  609.9 36.2 %fusion.32 = f32[1024,2048]{1,0:T(8,128)} fusion(bf16[2816,2048]{1,0:T(8,128)(2,1)} %param.18, f32[1024,2816]{1,0:T(8,128)} %fusion.31, bf16[1024,2048]{1,0:T(8,128)(2,1)} %split.6, bf16[2048,2816]{1,0:T(8,128)(2,1)} %param.17), kind=kOutput, calls=%fused_computation.103 | convolution fusion | flops 23639621632 | bytes 47185920 | tf_op jit(solution)/shard_map/dot_general | solution.py:215
  646.1 83.0 %expert_up.3.u_ref = bf16[20480,1408]{1,0:T(8,128)(2,1)} custom-call(s32[80]{0:T(128)} %broadcast_minimum_fusion.tile_exp, s32[81]{0:T(128)} %pad_add_fusion.2.tile_row, s32[45]{0:T(128)} %reshape.259.offs, s32[16800]{0:T(1024)} %reshape.260.owner, bf16[2048,16,128]{2,1,0:T(8,128)(2,1)} %bitcast.102, bf16[2048,16,128]{2,1,0:T(8,128)(2,1)} %collective-permute-done.5.x1, ...), custom_call_target="tpu_custom_call" | custom-call | flops 94489280512 | bytes 173015040 | tf_op jit(solution)/shard_map/expert_up/pallas_call | solution.py:171
  729.1 65.1 %expert_down.3 = (f32[2048,16,128]{2,1,0:T(8,128)}, f32[2048,16,128]{2,1,0:T(8,128)}) custom-call(s32[80]{0:T(128)} %broadcast_minimum_fusion.tile_exp, s32[81]{0:T(128)} %pad_add_fusion.2.tile_row, s32[45]{0:T(128)} %reshape.259.offs, s32[16800]{0:T(1024)} %reshape.260.owner, f32[16416]{0:T(1024)} %concatenate.42.gates, ...), custom_call_target="tpu_custom_call" | custom-call | flops 47244640256 | bytes 86507520 | tf_op jit(solution)/shard_map/expert_down/pallas_call | solution.py:189
  794.2 84.5 %collective-permute-start.6 = (f32[2048,16,128]{2,1,0:T(8,128)}, f32[2048,16,128]{2,1,0:T(8,128)}, u32[]{:S(2)}, u32[]{:S(2)}) collective-permute-start(f32[2048,16,128]{2,1,0:T(8,128)} %get-tuple-element.40), channel_id=1, source_target_pairs={{0,1},{1,0},{2,3},{3,2},{4,5},{5,4},{6,7},{7,6}} | collective-permute-start | bytes 50331656 | tf_op jit(solution)/shard_map/ppermute | solution.py:233
  878.7 52.6 %collective-permute-start.9 = (f32[1024,16,128]{2,1,0:T(8,128)}, f32[1024,16,128]{2,1,0:T(8,128)S(1)}, u32[]{:S(2)}, u32[]{:S(2)}) collective-permute-start(f32[1024,16,128]{2,1,0:T(8,128)} %add.189), channel_id=1, source_target_pairs={{0,2},{1,3},{2,0},{3,1},{4,6},{5,7},{6,4},{7,5}} | collective-permute-start | bytes 25165832 | tf_op jit(solution)/shard_map/ppermute | solution.py:228
  931.4 1.8 collective-permute-start.7
  933.4 179.5 %collective-permute-done.9 = f32[1024,16,128]{2,1,0:T(8,128)S(1)} collective-permute-done((f32[1024,16,128]{2,1,0:T(8,128)}, f32[1024,16,128]{2,1,0:T(8,128)S(1)}, u32[]{:S(2)}, u32[]{:S(2)}) %collective-permute-start.9) | collective-permute-done | bytes 8388640 | tf_op jit(solution)/shard_map/ppermute | solution.py:228
  1112.9 7.5 copy.50
  1120.4 172.1 %collective-permute-done.10 = f32[1024,16,128]{2,1,0:T(8,128)} collective-permute-done((f32[1024,16,128]{2,1,0:T(8,128)}, f32[1024,16,128]{2,1,0:T(8,128)}, u32[]{:S(2)}, u32[]{:S(2)}) %collective-permute-start.10) | collective-permute-done | bytes 8388640 | tf_op jit(solution)/shard_map/ppermute | solution.py:228
  1292.5 11.0 copy.49
  1303.6 11.7 add.193
  1315.3 30.0 %fusion.2 = bf16[2048,2048]{1,0:T(8,128)(2,1)} fusion(f32[256,8,16,128]{3,2,1,0:T(8,128)} %bitcast.93, f32[1024,2048]{1,0:T(8,128)} %collective-permute-done.8, f32[1024,2048]{1,0:T(8,128)} %collective-permute-done.7, f32[1024,2048]{1,0:T(8,128)} %bitcast.96, f32[1024,2048]{1,0:T(8,128)} %bitcast.95, f32[2048,2048]{1,0:T(8,128)} %fusion.3, ...), kind=kLoop, calls=%fused_computation.7 | loop fusion | flops 33554432 | bytes 83886080 | tf_op jit(solution)/shard_map/convert_element_type | solution.py:236
  (98 shorter events, 14.8 us)
Async XLA Ops:
  0.0 15.4 %copy-start.7 = (s32[1,60]{1,0:T(1,128)S(1)}, s32[1,60]{1,0:T(1,128)}, u32[]{:S(2)}) copy-start(s32[1,60]{1,0:T(1,128)} %param.15) | copy-start | bytes 724
  0.0 16.2 %copy-start.2 = (s32[2048,4]{0,1:T(4,128)S(1)}, s32[2048,4]{0,1:T(4,128)}, u32[]{:S(2)}) copy-start(s32[2048,4]{0,1:T(4,128)} %param.14) | copy-start | bytes 98308
  0.0 16.2 %copy-start.1 = (s32[2048,4]{0,1:T(4,128)S(1)}, s32[2048,4]{0,1:T(4,128)}, u32[]{:S(2)}) copy-start(s32[2048,4]{0,1:T(4,128)} %param.12) | copy-start | bytes 98308
  10.0 636.1 %collective-permute-start.5 = (bf16[2048,16,128]{2,1,0:T(8,128)(2,1)}, bf16[2048,16,128]{2,1,0:T(8,128)(2,1)}, u32[]{:S(2)}, u32[]{:S(2)}) collective-permute-start(bf16[2048,16,128]{2,1,0:T(8,128)(2,1)} %bitcast.100), channel_id=1, source_target_pairs={{0,1},{1,0},{2,3},{3,2},{4,5},{5,4},{6,7},{7,6}} | collective-permute-start | bytes 25165832 | tf_op jit(solution)/shard_map/ppermute | solution.py:131
  10.8 224.8 %collective-permute-start.1 = (bf16[2048,16,128]{2,1,0:T(8,128)(2,1)}, bf16[2048,16,128]{2,1,0:T(8,128)(2,1)}, u32[]{:S(2)}, u32[]{:S(2)}) collective-permute-start(bf16[2048,16,128]{2,1,0:T(8,128)(2,1)} %bitcast.101), channel_id=1, source_target_pairs={{0,2},{1,3},{2,0},{3,1},{4,6},{5,7},{6,4},{7,5}} | collective-permute-start | bytes 25165832 | tf_op jit(solution)/shard_map/ppermute | solution.py:130
  13.3 415.3 %collective-permute-start = (bf16[2048,2048]{1,0:T(8,128)(2,1)}, bf16[2048,2048]{1,0:T(8,128)(2,1)}, u32[]{:S(2)}, u32[]{:S(2)}) collective-permute-start(bf16[2048,2048]{1,0:T(8,128)(2,1)} %param.11), channel_id=1, source_target_pairs={{0,4},{4,0},{1,5},{5,1},{2,6},{6,2},{3,7},{7,3}} | collective-permute-start | bytes 25165832 | tf_op jit(solution)/shard_map/ppermute | solution.py:133
  48.8 220.1 %all-to-all-start = ((s32[4,15,560]{2,1,0:T(8,128)}), s32[4,15,560]{2,1,0:T(8,128)}, u32[]{:S(2)}, u32[]{:S(2)}) async-start(s32[4,15,560]{2,1,0:T(8,128)} %pad_add_fusion), calls=%async_computation | async-start | bytes 327680 | tf_op jit(solution)/shard_map/all_to_all | solution.py:141
  52.8 31.9 %copy-start.3 = (f32[2048,4]{0,1:T(4,128)S(1)}, f32[2048,4]{0,1:T(4,128)}, u32[]{:S(2)}) copy-start(f32[2048,4]{0,1:T(4,128)} %param.13) | copy-start | bytes 98308
  200.5 35.1 %copy-start.4 = (s32[1024]{0:T(1024)}, s32[1024]{0:T(1024)S(1)}, u32[]{:S(2)}) copy-start(s32[1024]{0:T(1024)S(1)} %pad_clamp_fusion) | copy-start | bytes 12292
  201.2 34.5 %copy-start.5 = (pred[4]{0:T(512)(128)(4,1)}, pred[4]{0:T(512)(128)(4,1)S(1)}, u32[]{:S(2)}) copy-start(pred[4]{0:T(512)(128)(4,1)S(1)} %compare_and_fusion) | copy-start | bytes 16
  235.6 44.0 %collective-permute-start.2 = (bf16[2048,16,128]{2,1,0:T(8,128)(2,1)}, bf16[2048,16,128]{2,1,0:T(8,128)(2,1)}, u32[]{:S(2)}, u32[]{:S(2)}) collective-permute-start(bf16[2048,16,128]{2,1,0:T(8,128)(2,1)} %collective-permute-done.1.x0), channel_id=1, source_target_pairs={{0,1},{1,0},{2,3},{3,2},{4,5},{5,4},{6,7},{7,6}} | collective-permute-start | bytes 25165832 | tf_op jit(solution)/shard_map/ppermute | solution.py:132
  237.0 33.5 %copy-start.6 = (pred[4]{0:T(512)(128)(4,1)S(1)}, pred[4]{0:T(512)(128)(4,1)}, u32[]{:S(2)}) copy-start(pred[4]{0:T(512)(128)(4,1)} %copy-done.5) | copy-start | bytes 16
  433.4 138.4 %collective-permute-start.3 = (f32[1024,16,128]{2,1,0:T(8,128)}, f32[1024,16,128]{2,1,0:T(8,128)}, u32[]{:S(2)}, u32[]{:S(2)}) collective-permute-start(f32[1024,16,128]{2,1,0:T(8,128)} %get-tuple-element.33), channel_id=1, source_target_pairs={{0,1},{1,0},{2,3},{3,2},{4,5},{5,4},{6,7},{7,6}} | collective-permute-start | bytes 25165832 | tf_op jit(solution)/shard_map/ppermute | solution.py:223
  517.3 64.7 %collective-permute-start.4 = (f32[1024,16,128]{2,1,0:T(8,128)}, f32[1024,16,128]{2,1,0:T(8,128)}, u32[]{:S(2)}, u32[]{:S(2)}) collective-permute-start(f32[1024,16,128]{2,1,0:T(8,128)} %get-tuple-element.36), channel_id=1, source_target_pairs={{0,1},{1,0},{2,3},{3,2},{4,5},{5,4},{6,7},{7,6}} | collective-permute-start | bytes 25165832 | tf_op jit(solution)/shard_map/ppermute | solution.py:223
  581.9 10.3 copy-start
  794.2 509.3 %collective-permute-start.6 = (f32[2048,16,128]{2,1,0:T(8,128)}, f32[2048,16,128]{2,1,0:T(8,128)}, u32[]{:S(2)}, u32[]{:S(2)}) collective-permute-start(f32[2048,16,128]{2,1,0:T(8,128)} %get-tuple-element.40), channel_id=1, source_target_pairs={{0,1},{1,0},{2,3},{3,2},{4,5},{5,4},{6,7},{7,6}} | collective-permute-start | bytes 50331656 | tf_op jit(solution)/shard_map/ppermute | solution.py:233
  878.7 234.1 %collective-permute-start.9 = (f32[1024,16,128]{2,1,0:T(8,128)}, f32[1024,16,128]{2,1,0:T(8,128)S(1)}, u32[]{:S(2)}, u32[]{:S(2)}) collective-permute-start(f32[1024,16,128]{2,1,0:T(8,128)} %add.189), channel_id=1, source_target_pairs={{0,2},{1,3},{2,0},{3,1},{4,6},{5,7},{6,4},{7,5}} | collective-permute-start | bytes 25165832 | tf_op jit(solution)/shard_map/ppermute | solution.py:228
  931.3 361.2 %collective-permute-start.10 = (f32[1024,16,128]{2,1,0:T(8,128)}, f32[1024,16,128]{2,1,0:T(8,128)}, u32[]{:S(2)}, u32[]{:S(2)}) collective-permute-start(f32[1024,16,128]{2,1,0:T(8,128)} %add.190), channel_id=1, source_target_pairs={{0,2},{1,3},{2,0},{3,1},{4,6},{5,7},{6,4},{7,5}} | collective-permute-start | bytes 25165832 | tf_op jit(solution)/shard_map/ppermute | solution.py:228
  931.4 383.9 %collective-permute-start.7 = (f32[1024,2048]{1,0:T(8,128)}, f32[1024,2048]{1,0:T(8,128)}, u32[]{:S(2)}, u32[]{:S(2)}) collective-permute-start(f32[1024,2048]{1,0:T(8,128)} %fusion.8), channel_id=1, source_target_pairs={{0,4},{4,0},{1,5},{5,1},{2,6},{6,2},{3,7},{7,3}} | collective-permute-start | bytes 25165832 | tf_op jit(solution)/shard_map/ppermute | solution.py:231
  933.2 382.1 %collective-permute-start.8 = (f32[1024,2048]{1,0:T(8,128)}, f32[1024,2048]{1,0:T(8,128)}, u32[]{:S(2)}, u32[]{:S(2)}) collective-permute-start(f32[1024,2048]{1,0:T(8,128)} %fusion.32), channel_id=1, source_target_pairs={{0,4},{4,0},{1,5},{5,1},{2,6},{6,2},{3,7},{7,3}} | collective-permute-start | bytes 25165832 | tf_op jit(solution)/shard_map/ppermute | solution.py:231
  1112.9 190.7 %slice-start = ((s8[16777216]{0:T(1024)(128)(4,1)}), s8[4194304]{0:T(1024)(128)(4,1)S(1)}, s32[]{:S(2)}) async-start(s8[16777216]{0:T(1024)(128)(4,1)} %bitcast.97), calls=%async_computation.1 | async-start | bytes 8388608
  1112.9 190.7 %slice-start.1 = ((s8[16777216]{0:T(1024)(128)(4,1)}), s8[4194304]{0:T(1024)(128)(4,1)S(1)}, s32[]{:S(2)}) async-start(s8[16777216]{0:T(1024)(128)(4,1)} %bitcast.97), calls=%async_computation.2 | async-start | bytes 8388608
  1292.5 11.0 slice-start.2
  1292.5 11.0 slice-start.3

commit v2 on v1

--- a/solution.py
+++ b/solution.py
@@ -30,12 +30,14 @@
     return lo - start, jnp.maximum(hi - lo, 0), lo - base
 
 
-def up_kernel(n_tok, top_k, n_local, table_cols, tile_exp, tile_row, offs, owner, x0, x1, w1_ref, w3_ref, u_ref, tok_vmem, rows_vmem, sems):
+def up_kernel(n_tok, top_k, n_local, table_cols, tile_exp, tile_row, offs, owner, *refs):
+    *parts, w1_ref, w3_ref, u_ref, tok_vmem, rows_vmem, sems = refs
     step = pl.program_id(0)
 
     @pl.when(step == 0)
     def _():
-        copies = [pltpu.make_async_copy(src, tok_vmem.at[pl.ds(q * n_tok, n_tok)], sems.at[q]) for q, src in enumerate((x0, x1))]
+        rows = PAIR * n_tok // len(parts)
+        copies = [pltpu.make_async_copy(src, tok_vmem.at[pl.ds(i * rows, rows)], sems.at[i]) for i, src in enumerate(parts)]
         for copy in copies:
             copy.start()
         for copy in copies:
@@ -63,17 +65,17 @@
 
 
 def down_kernel(n_tok, top_k, n_local, table_cols, tile_exp, tile_row, offs, owner, gates, u_ref, w2_ref, *refs):
-    *outs, acc, tile_vmem, sems = refs
+    *outs, acc, tile_vmem, stage, sems = refs
     step = pl.program_id(0)
     cols = w2_ref.shape[2] // LANES
 
     @pl.when(step == 0)
     def _():
         def clear(g, carry):
-            acc[pl.ds(g * 8, 8)] = jnp.zeros((8, cols, LANES), jnp.float32)
+            acc[pl.ds(pl.multiple_of(g * 128, 128), 128), :] = jnp.zeros((128, LANES), jnp.float32)
             return carry
 
-        lax.fori_loop(0, PAIR * n_tok // 8, clear, 0)
+        lax.fori_loop(0, PAIR * n_tok * cols // 128, clear, 0)
 
     @pl.when(step < tile_row[pl.num_programs(0)])
     def _():
@@ -89,12 +91,12 @@
 
             def scatter(g, carry):
                 copy_ids = [owner[src + g * UNROLL + j] for j in range(UNROLL)]
-                toks = [token_of(copy_id, top_k) for copy_id in copy_ids]
+                toks = [pl.ds(pl.multiple_of(token_of(copy_id, top_k) * cols, cols), cols) for copy_id in copy_ids]
                 firsts = [pl.multiple_of((dst + g * UNROLL + j) * cols, cols) for j in range(UNROLL)]
                 vals = [tile_vmem[pl.ds(firsts[j], cols), :] * gates[copy_ids[j]] for j in range(UNROLL)]
-                olds = [acc[t] for t in toks]
+                olds = [acc[t, :] for t in toks]
                 for j in range(UNROLL):
-                    acc[toks[j]] = olds[j] + vals[j]
+                    acc[toks[j], :] = olds[j] + vals[j]
                 return carry
 
             lax.fori_loop(0, lax.div(count, UNROLL), scatter, 0)
@@ -102,11 +104,27 @@
     @pl.when(step == pl.num_programs(0) - 1)
     def _():
         rows = PAIR * n_tok // len(outs)
-        copies = [pltpu.make_async_copy(acc.at[pl.ds(i * rows, rows)], dst, sems.at[i]) for i, dst in enumerate(outs)]
-        for copy in copies:
-            copy.start()
-        for copy in copies:
-            copy.wait()
+        block = stage.shape[1]
+        for i, dst in enumerate(outs):
+
+            def flush(g, carry):
+                for half in range(2):
+                    copy = pltpu.make_async_copy(stage.at[half], dst.at[pl.ds(pl.multiple_of((g * 2 + half) * block, block), block), :], sems.at[half])
+
+                    @pl.when(g > 0)
+                    def _():
+                        copy.wait()
+
+                    first = pl.multiple_of((i * rows + (g * 2 + half) * block) * cols, block * cols)
+                    for b in range(block // 8):
+                        for c in range(cols):
+                            stage[half, b * 8 : (b + 1) * 8, c * LANES : (c + 1) * LANES] = acc[pl.ds(first + b * 8 * cols + c, 8, stride=cols), :]
+                    copy.start()
+                return carry
+
+            lax.fori_loop(0, rows // (2 * block), flush, 0)
+            for half in range(2):
+                pltpu.make_async_copy(stage.at[half], dst.at[pl.ds(half * block, block), :], sems.at[half]).wait()
 
 
 def solution(mesh):
@@ -128,21 +146,21 @@
 
         toks3 = tokens.reshape(n_tok, d_model // LANES, LANES)
         x_chip = lax.ppermute(toks3, "ep", chip_swap)
+        peer_rows = [lax.ppermute(part, "tp", [(0, 1), (1, 0)]) for part in jnp.split(tokens, 2)]
         x_core = lax.ppermute(toks3, "ep", core_swap)
         x_diag = lax.ppermute(x_chip, "ep", core_swap)
-        peer_tokens = lax.ppermute(tokens, "tp", [(0, 1), (1, 0)])
 
         slots = jnp.where((slot_ids >= 0) & (slot_ids < capacity), slot_ids, table_cols)
         copy_ids = jnp.arange(n_tok * top_k, dtype=jnp.int32)
         dest = jnp.where(slots < capacity, expert_ids * table_cols + slots, n_exp * table_cols).reshape(-1)
         owner = jnp.zeros((n_exp * table_cols,), jnp.int32).at[dest].set(copy_ids, mode="drop").reshape(n_exp, table_cols)
-        owner = jnp.concatenate([owner[:, :-1], send_counts[0][:, None]], axis=1)
-        order = rank ^ jnp.arange(ep_size, dtype=jnp.int32)
-        owner = lax.all_to_all(owner.reshape(ep_size, n_local, table_cols), "ep", 0, 0, tiled=True)
-        owner = jnp.take(owner, order, axis=0)
-        gates = lax.all_gather(gate_vals.reshape(-1), "ep", axis=0)
-        gates = jnp.take(gates, order, axis=0)
-
+        owner = jnp.concatenate([owner[:, :-1], send_counts[0][:, None]], axis=1).reshape(ep_size, n_local * table_cols)
+        flat_gates = jnp.broadcast_to(gate_vals.reshape(1, -1), (ep_size, n_tok * top_k))
+        message = jnp.concatenate([owner.astype(jnp.float32), flat_gates], axis=1)
+        message = lax.all_to_all(message, "ep", 0, 0, tiled=True)
+        message = jnp.take(message, rank ^ jnp.arange(ep_size, dtype=jnp.int32), axis=0)
+        owner = message[:, : n_local * table_cols].astype(jnp.int32).reshape(ep_size, n_local, table_cols)
+        gates = message[:, n_local * table_cols :]
         counts = jnp.minimum(owner[:, :, -1], capacity)
 
         any_spec = pl.BlockSpec(memory_space=pl.ANY)
@@ -166,26 +184,26 @@
             gate = jnp.append(gates[first : first + PAIR].reshape(-1), jnp.zeros((UNROLL * top_k,), jnp.float32))
             return tile_exp, tile_row, offs.T.reshape(-1), rows, gate
 
-        def experts(planned, rows0, rows1, n_out):
+        def experts(planned, parts, n_out):
             tile_exp, tile_row, offs, rows, gate = planned
             hidden = pl.pallas_call(
                 functools.partial(up_kernel, n_tok, top_k, n_local, table_cols),
                 grid_spec=pltpu.PrefetchScalarGridSpec(
                     num_scalar_prefetch=4,
                     grid=(max_tiles,),
-                    in_specs=[any_spec] * PAIR + [pl.BlockSpec((1, d_model, d_ff), lambda i, te, tr, of, ow: (te[i], 0, 0))] * 2,
+                    in_specs=[any_spec] * len(parts) + [pl.BlockSpec((1, d_model, d_ff), lambda i, te, tr, of, ow: (te[i], 0, 0))] * 2,
                     out_specs=pl.BlockSpec((TILE, d_ff), lambda i, te, tr, of, ow: (jnp.minimum(i, tr[max_tiles] - 1), 0)),
                     scratch_shapes=[
                         pltpu.VMEM((PAIR * n_tok + UNROLL, d_model // LANES, LANES), jnp.bfloat16),
                         pltpu.VMEM((TILE, d_model // LANES, LANES), jnp.bfloat16),
-                        pltpu.SemaphoreType.DMA((PAIR,)),
+                        pltpu.SemaphoreType.DMA((len(parts),)),
                     ],
                 ),
                 out_shape=jax.ShapeDtypeStruct((max_tiles * TILE, d_ff), jnp.bfloat16),
                 compiler_params=pltpu.CompilerParams(vmem_limit_bytes=60 * 2**20, dimension_semantics=("arbitrary",)),
                 cost_estimate=pl.CostEstimate(flops=4 * avg_rows * d_model * d_ff, bytes_accessed=4 * n_local * d_model * d_ff, transcendentals=0),
                 name="expert_up",
-            )(tile_exp, tile_row, offs, rows, rows0, rows1, expert_w1, expert_w3)
+            )(tile_exp, tile_row, offs, rows, *parts, expert_w1, expert_w3)
             return pl.pallas_call(
                 functools.partial(down_kernel, n_tok, top_k, n_local, table_cols),
                 grid_spec=pltpu.PrefetchScalarGridSpec(
@@ -197,12 +215,13 @@
                     ],
                     out_specs=[any_spec] * n_out,
                     scratch_shapes=[
-                        pltpu.VMEM((PAIR * n_tok + UNROLL, d_model // LANES, LANES), jnp.float32),
+                        pltpu.VMEM(((PAIR * n_tok + UNROLL) * d_model // LANES, LANES), jnp.float32),
                         pltpu.VMEM((TILE * d_model // LANES, LANES), jnp.float32),
-                        pltpu.SemaphoreType.DMA((n_out,)),
+                        pltpu.VMEM((2, min(64, n_tok // 4), d_model), jnp.float32),
+                        pltpu.SemaphoreType.DMA((2,)),
                     ],
                 ),
-                out_shape=[jax.ShapeDtypeStruct((PAIR * n_tok // n_out, d_model // LANES, LANES), jnp.float32)] * n_out,
+                out_shape=[jax.ShapeDtypeStruct((PAIR * n_tok // n_out, d_model), jnp.float32)] * n_out,
                 compiler_params=pltpu.CompilerParams(vmem_limit_bytes=60 * 2**20, dimension_semantics=("arbitrary",)),
                 cost_estimate=pl.CostEstimate(flops=2 * avg_rows * d_model * d_ff, bytes_accessed=2 * n_local * d_model * d_ff, transcendentals=0),
                 name="expert_down",
@@ -216,24 +235,22 @@
 
         far_plan, near_plan = plan(PAIR), plan(0)
         own_part = shared_part(tokens)
-        tile_exp, own_part = lax.optimization_barrier((far_plan[0], own_part))
-        far_sums = experts((tile_exp, *far_plan[1:]), x_chip, x_diag, 4)
-        peer_tokens, *far_sums = lax.optimization_barrier((peer_tokens, *far_sums))
-        peer_rows = jnp.split(peer_tokens, 2)
+        peer_rows[0], own_part = lax.optimization_barrier((peer_rows[0], own_part))
+        peer_0 = shared_part(peer_rows[0])
+        tile_exp, peer_0 = lax.optimization_barrier((far_plan[0], peer_0))
+        far_sums = experts((tile_exp, *far_plan[1:]), (x_chip, x_diag), 4)
+        peer_rows[1], *far_sums = lax.optimization_barrier((peer_rows[1], *far_sums))
         swapped = [lax.ppermute(part, "ep", core_swap) for part in far_sums[2:]]
-        peer_0 = shared_part(peer_rows[0])
-        swapped[0], peer_0 = lax.optimization_barrier((swapped[0], peer_0))
         chip_sums = [mine + theirs for mine, theirs in zip(far_sums[:2], swapped)]
-        rows_1, *chip_sums = lax.optimization_barrier((peer_rows[1], *chip_sums))
+        peer_1 = shared_part(peer_rows[1])
+        tile_exp, peer_1, *chip_sums = lax.optimization_barrier((near_plan[0], peer_1, *chip_sums))
         back = [lax.ppermute(part, "ep", chip_swap) for part in chip_sums]
-        peer_1 = shared_part(rows_1)
-        tile_exp, peer_1 = lax.optimization_barrier((near_plan[0], peer_1))
         peer_back = [lax.ppermute(part, "tp", [(0, 1), (1, 0)]) for part in (peer_0, peer_1)]
-        own, core = experts((tile_exp, *near_plan[1:]), toks3, x_core, 2)
-        near = (own + lax.ppermute(core, "ep", core_swap)).reshape(n_tok, d_model)
-        kept = tokens.astype(jnp.float32) + own_part + near
-        routed = jnp.concatenate([part.reshape(-1, d_model) for part in back])
-        return (kept + jnp.concatenate(peer_back) + routed).astype(jnp.bfloat16)
+        own, core = experts((tile_exp, *near_plan[1:]), (toks3, x_core), 2)
+        near = own + lax.ppermute(core, "ep", core_swap)
+        kept = tokens.astype(jnp.float32) + own_part + jnp.concatenate(peer_back) + near
+        kept, *back = lax.optimization_barrier((kept, *back))
+        return (kept + jnp.concatenate(back)).astype(jnp.bfloat16)
 
     return jax.shard_map(
         layer_body,

time: 1350 us -> 1320 us (0.978)
  the two profiles are of different devices: /device:TPU:0 before, /device:TPU:6 now
where the time goes in v2:
time: 1320 us
  Pallas kernels  566 us (43%)
  waiting for transfers between devices  395 us (30%)
  matrix products  209 us (16%)
  other arithmetic  75.6 us (6%)
  local copies, waits for them, and re-layouts  58.4 us (4%)
    ppermute x4, waiting for transfers between devices, layer_body(): lax.ppermute(part, 'tp', [(0, 1), (1, 0)])  359 us
    pallas_call x2, Pallas kernels, experts(): pl.pallas_call(functools.partial(up_kernel, n_tok, top_k, n_local, table_...  291 us
    pallas_call x2, Pallas kernels, experts(): pl.pallas_call(functools.partial(down_kernel, n_tok, top_k, n_local, tabl...  275 us
    dot_general x3, matrix products, shared_part(): return jnp.dot(shared_hidden, shared_w2, preferred_element_type=jnp.float32)  106 us
    dot_general x3, matrix products, shared_part(): pre_gate = jnp.dot(rows, shared_w1, preferred_element_type=jnp.float32)  69.3 us
    all_to_all x1, waiting for transfers between devices, layer_body(): message = lax.all_to_all(message, 'ep', 0, 0, tiled=True)  36.3 us
    dot_general x1, matrix products, shared_part(): pre_up = jnp.dot(rows, shared_w3, preferred_element_type=jnp.float32)  34.3 us
    add x1, other arithmetic, layer_body(): tokens.astype(jnp.float32) + own_part + jnp.concatenate(peer_back) + near  31.9 us
  transfers between devices with their start and end apart: 13, of which 3 were waited for; matrix products, arithmetic and copies ran while one was open for 24% of the time, Pallas kernels for 21%

profile of v2, /device:TPU:6, one launch (start us, length us, event | category | flops | bytes accessed | tf_op | source)
XLA Modules:
  0.0 1319.0 jit_solution(7392934460252181404)
XLA Ops:
  0.0 10.0 copy.38
  11.1 0.7 reshape.257
  11.9 30.5 %scatter_custom_fusion = s32[33600]{0:T(1024)S(1)} fusion(s32[8192]{0:T(1024)S(1)} %bitcast.78, s32[8192]{0:T(1024)S(1)} %iota.39, s32[]{:T(128)} %constant.121.clone.1), kind=kCustom, calls=%fused_computation.22 | custom fusion | bytes 134404 | tf_op jit(solution)/shard_map/scatter | solution.py:156
  43.9 0.9 all_to_all.8
  44.8 5.8 all-to-all-start
  50.6 6.2 fusion.24
  57.3 1.5 collective-permute-start.2
  59.4 0.7 broadcast_in_dim.84
  60.2 0.7 add.190
  60.9 31.9 %fusion.30 = f32[2048,2816]{1,0:T(8,128)} fusion(bf16[2048,2048]{1,0:T(8,128)(2,1)} %param.11, bf16[2048,2816]{1,0:T(8,128)(2,1)} %param.16), kind=kOutput, calls=%fused_computation.100 | convolution fusion | flops 23622320128 | bytes 42991616 | tf_op jit(solution)/shard_map/dot_general | solution.py:231
  92.8 34.3 %multiply_convert_fusion.clone.4 = bf16[2048,2816]{1,0:T(8,128)(2,1)} fusion(f32[2048,2816]{1,0:T(8,128)} %fusion.30, bf16[2048,2048]{1,0:T(8,128)(2,1)} %param.11, bf16[2048,2816]{1,0:T(8,128)(2,1)} %param.17), kind=kOutput, calls=%fused_computation.2.clone.clone.clone.1 | convolution fusion | flops 23656923136 | bytes 54525952 | tf_op jit(solution)/shard_map/dot_general | solution.py:232
  127.1 32.6 %fusion.2 = f32[2048,2048]{1,0:T(8,128)} fusion(bf16[2816,2048]{1,0:T(8,128)(2,1)} %param.18, bf16[2048,2816]{1,0:T(8,128)(2,1)} %multiply_convert_fusion.clone.4), kind=kOutput, calls=%fused_computation.9 | convolution fusion | flops 23622320128 | bytes 39845888 | tf_op jit(solution)/shard_map/dot_general | solution.py:234
  159.8 36.3 %all-to-all-done = f32[4,1,16592]{2,1,0:T(1,128)} async-done(((f32[4,1,16592]{2,1,0:T(1,128)}), f32[4,1,16592]{2,1,0:T(1,128)}, u32[]{:S(2)}, u32[]{:S(2)}) %all-to-all-start) | async-done | bytes 265504 | tf_op jit(solution)/shard_map/all_to_all | solution.py:160
  196.0 1.0 copy.41
  197.1 0.7 gather_fusion
  207.4 0.7 add_select_fusion
  208.1 18.7 %fusion.31 = f32[1024,2816]{1,0:T(8,128)} fusion(bf16[1024,2048]{1,0:T(8,128)(2,1)} %collective-permute-done, bf16[2048,2816]{1,0:T(8,128)(2,1)} %param.16), kind=kOutput, calls=%fused_computation.101 | convolution fusion | flops 11811160064 | bytes 27262976 | tf_op jit(solution)/shard_map/dot_general | solution.py:231
  226.8 36.4 %fusion.3 = f32[1024,2048]{1,0:T(8,128)} fusion(bf16[2816,2048]{1,0:T(8,128)(2,1)} %param.18, f32[1024,2816]{1,0:T(8,128)} %fusion.31, bf16[1024,2048]{1,0:T(8,128)(2,1)} %collective-permute-done, bf16[2048,2816]{1,0:T(8,128)(2,1)} %param.17), kind=kOutput, calls=%fused_computation.10 | convolution fusion | flops 23639621632 | bytes 47185920 | tf_op jit(solution)/shard_map/dot_general | solution.py:234
  263.3 145.6 %expert_up.2.u_ref = bf16[20480,1408]{1,0:T(8,128)(2,1)} custom-call(s32[80]{0:T(128)} %broadcast_minimum_fusion.1.tile_exp, s32[81]{0:T(128)} %pad_add_fusion.tile_row, s32[45]{0:T(128)} %reshape.261.offs, s32[16800]{0:T(1024)} %get-tuple-element.60.owner, bf16[2048,16,128]{2,1,0:T(8,128)(2,1)} %collective-permute-done.3.refs_0_, ...), custom_call_target="tpu_custom_call" | custom-call | flops 94489280512 | bytes 173015040 | tf_op jit(solution)/shard_map/expert_up/pallas_call | solution.py:189
  408.9 137.8 %expert_down.2 = (f32[1024,2048]{1,0:T(8,128)}, f32[1024,2048]{1,0:T(8,128)}, f32[1024,2048]{1,0:T(8,128)}, f32[1024,2048]{1,0:T(8,128)}) custom-call(s32[80]{0:T(128)} %broadcast_minimum_fusion.1.tile_exp, s32[81]{0:T(128)} %pad_add_fusion.tile_row, s32[45]{0:T(128)} %reshape.261.offs, s32[16800]{0:T(1024)} %get-tuple-element.60.owner, ...), custom_call_target="tpu_custom_call" | custom-call | flops 47244640256 | bytes 86507520 | tf_op jit(solution)/shard_map/expert_down/pallas_call | solution.py:207
  547.2 18.7 %fusion.32 = f32[1024,2816]{1,0:T(8,128)} fusion(bf16[1024,2048]{1,0:T(8,128)(2,1)} %collective-permute-done.2, bf16[2048,2816]{1,0:T(8,128)(2,1)} %param.16), kind=kOutput, calls=%fused_computation.102 | convolution fusion | flops 11811160064 | bytes 27262976 | tf_op jit(solution)/shard_map/dot_general | solution.py:231
  565.9 36.6 %fusion.4 = f32[1024,2048]{1,0:T(8,128)} fusion(bf16[2816,2048]{1,0:T(8,128)(2,1)} %param.18, f32[1024,2816]{1,0:T(8,128)} %fusion.32, bf16[1024,2048]{1,0:T(8,128)(2,1)} %collective-permute-done.2, bf16[2048,2816]{1,0:T(8,128)(2,1)} %param.17), kind=kOutput, calls=%fused_computation.11 | convolution fusion | flops 23639621632 | bytes 47185920 | tf_op jit(solution)/shard_map/dot_general | solution.py:234
  602.6 11.8 add.195
  614.4 11.8 add.196
  626.1 145.6 %expert_up.3.u_ref = bf16[20480,1408]{1,0:T(8,128)(2,1)} custom-call(s32[80]{0:T(128)} %broadcast_minimum_fusion.tile_exp, s32[81]{0:T(128)} %pad_add_fusion.1.tile_row, s32[45]{0:T(128)} %reshape.265.offs, s32[16800]{0:T(1024)} %get-tuple-element.59.owner, bf16[2048,16,128]{2,1,0:T(8,128)(2,1)} %bitcast.74, ...), custom_call_target="tpu_custom_call" | custom-call | flops 94489280512 | bytes 173015040 | tf_op jit(solution)/shard_map/expert_up/pallas_call | solution.py:189
  771.7 136.9 %expert_down.3 = (f32[2048,2048]{1,0:T(8,128)}, f32[2048,2048]{1,0:T(8,128)}) custom-call(s32[80]{0:T(128)} %broadcast_minimum_fusion.tile_exp, s32[81]{0:T(128)} %pad_add_fusion.1.tile_row, s32[45]{0:T(128)} %reshape.265.offs, s32[16800]{0:T(1024)} %get-tuple-element.59.owner, f32[16416]{0:T(1024)} %concatenate.40.gates, ...), custom_call_target="tpu_custom_call" | custom-call | flops 47244640256 | bytes 86507520 | tf_op jit(solution)/shard_map/expert_down/pallas_call | solution.py:207
  908.8 1.9 collective-permute-start.7
  910.7 2.0 collective-permute-start.11
  912.7 179.6 %collective-permute-done.1 = f32[1024,2048]{1,0:T(8,128)} collective-permute-done((f32[1024,2048]{1,0:T(8,128)}, f32[1024,2048]{1,0:T(8,128)}, u32[]{:S(2)}, u32[]{:S(2)}) %collective-permute-start.1) | collective-permute-done | bytes 8388640 | tf_op jit(solution)/shard_map/ppermute | solution.py:248
  1092.3 179.3 %collective-permute-done.7 = f32[1024,2048]{1,0:T(8,128)} collective-permute-done((f32[1024,2048]{1,0:T(8,128)}, f32[1024,2048]{1,0:T(8,128)}, u32[]{:S(2)}, u32[]{:S(2)}) %collective-permute-start.7) | collective-permute-done | bytes 8388640 | tf_op jit(solution)/shard_map/ppermute | solution.py:248
  1271.6 31.9 %fusion = f32[2048,2048]{1,0:T(8,128)} fusion(f32[1024,2048]{1,0:T(8,128)} %collective-permute-done.7, f32[1024,2048]{1,0:T(8,128)} %collective-permute-done.1, f32[2048,2048]{1,0:T(8,128)} %get-tuple-element.42, f32[2048,2048]{1,0:T(8,128)} %collective-permute-done.9, f32[2048,2048]{1,0:T(8,128)} %fusion.2, bf16[2048,2048]{1,0:T(8,128)(2,1)} %param.11), kind=kLoop, calls=%fused_computation.4 | loop fusion | flops 25165824 | bytes 92274688 | tf_op jit(solution)/shard_map/add | solution.py:251
  1303.5 15.3 %fusion.1 = bf16[2048,2048]{1,0:T(8,128)(2,1)} fusion(f32[2048,2048]{1,0:T(8,128)} %fusion, f32[1024,2048]{1,0:T(8,128)} %collective-permute-done.11, f32[1024,2048]{1,0:T(8,128)} %collective-permute-done.10), kind=kLoop, calls=%fused_computation.6 | loop fusion | flops 12582912 | bytes 41943040 | tf_op jit(solution)/shard_map/convert_element_type | solution.py:253
  (95 shorter events, 12.9 us)
Async XLA Ops:
  0.0 10.5 copy-start.5
  0.0 10.6 copy-start.3
  0.0 10.6 copy-start.2
  0.0 42.7 %copy-start.4 = (f32[2048,4]{0,1:T(4,128)S(1)}, f32[2048,4]{0,1:T(4,128)}, u32[]{:S(2)}) copy-start(f32[2048,4]{0,1:T(4,128)} %param.13) | copy-start | bytes 98308
  10.0 616.1 %collective-permute-start.8 = (bf16[2048,16,128]{2,1,0:T(8,128)(2,1)}, bf16[2048,16,128]{2,1,0:T(8,128)(2,1)}, u32[]{:S(2)}, u32[]{:S(2)}) collective-permute-start(bf16[2048,16,128]{2,1,0:T(8,128)(2,1)} %bitcast.72), channel_id=1, source_target_pairs={{0,1},{1,0},{2,3},{3,2},{4,5},{5,4},{6,7},{7,6}} | collective-permute-start | bytes 25165832 | tf_op jit(solution)/shard_map/ppermute | solution.py:150
  10.0 198.1 %collective-permute-start.3 = (bf16[2048,16,128]{2,1,0:T(8,128)(2,1)}, bf16[2048,16,128]{2,1,0:T(8,128)(2,1)}, u32[]{:S(2)}, u32[]{:S(2)}) collective-permute-start(bf16[2048,16,128]{2,1,0:T(8,128)(2,1)} %bitcast.73), channel_id=1, source_target_pairs={{0,2},{1,3},{2,0},{3,1},{4,6},{5,7},{6,4},{7,5}} | collective-permute-start | bytes 25165832 | tf_op jit(solution)/shard_map/ppermute | solution.py:148
  44.8 151.2 %all-to-all-start = ((f32[4,1,16592]{2,1,0:T(1,128)}), f32[4,1,16592]{2,1,0:T(1,128)}, u32[]{:S(2)}, u32[]{:S(2)}) async-start(f32[4,1,16592]{2,1,0:T(1,128)} %all_to_all.8), calls=%async_computation | async-start | bytes 532480 | tf_op jit(solution)/shard_map/all_to_all | solution.py:160
  56.8 151.3 %collective-permute-start = (bf16[1024,2048]{1,0:T(8,128)(2,1)}, bf16[1024,2048]{1,0:T(8,128)(2,1)}, u32[]{:S(2)}, u32[]{:S(2)}) collective-permute-start(bf16[1024,2048]{1,0:T(8,128)(2,1)} %get-tuple-element.55), channel_id=1, source_target_pairs={{0,4},{4,0},{1,5},{5,1},{2,6},{6,2},{3,7},{7,3}} | collective-permute-start | bytes 12582920 | tf_op jit(solution)/shard_map/ppermute | solution.py:149
  57.3 489.3 %collective-permute-start.2 = (bf16[1024,2048]{1,0:T(8,128)(2,1)}, bf16[1024,2048]{1,0:T(8,128)(2,1)}, u32[]{:S(2)}, u32[]{:S(2)}) collective-permute-start(bf16[1024,2048]{1,0:T(8,128)(2,1)} %get-tuple-element.56), channel_id=1, source_target_pairs={{0,4},{4,0},{1,5},{5,1},{2,6},{6,2},{3,7},{7,3}} | collective-permute-start | bytes 12582920 | tf_op jit(solution)/shard_map/ppermute | solution.py:149
  127.1 32.6 %copy-start.6 = (s32[4]{0:T(128)S(1)}, s32[4]{0:T(128)}, u32[]{:S(2)}) copy-start(s32[4]{0:T(128)} %fusion.18) | copy-start | bytes 52
  127.1 80.3 %copy-start = (s32[16800]{0:T(1024)S(1)}, s32[16800]{0:T(1024)}, u32[]{:S(2)}) copy-start(s32[16800]{0:T(1024)} %broadcast_in_dim.84) | copy-start | bytes 201604
  127.1 80.3 %copy-start.1 = (s32[16800]{0:T(1024)S(1)}, s32[16800]{0:T(1024)}, u32[]{:S(2)}) copy-start(s32[16800]{0:T(1024)} %add.190) | copy-start | bytes 201604
  208.1 55.2 %collective-permute-start.4 = (bf16[2048,16,128]{2,1,0:T(8,128)(2,1)}, bf16[2048,16,128]{2,1,0:T(8,128)(2,1)}, u32[]{:S(2)}, u32[]{:S(2)}) collective-permute-start(bf16[2048,16,128]{2,1,0:T(8,128)(2,1)} %collective-permute-done.3.refs_0_), channel_id=1, source_target_pairs={{0,1},{1,0},{2,3},{3,2},{4,5},{5,4},{6,7},{7,6}} | collective-permute-start | bytes 25165832 | tf_op jit(solution)/shard_map/ppermute | solution.py:151
  546.7 55.9 %collective-permute-start.5 = (f32[1024,2048]{1,0:T(8,128)}, f32[1024,2048]{1,0:T(8,128)}, u32[]{:S(2)}, u32[]{:S(2)}) collective-permute-start(f32[1024,2048]{1,0:T(8,128)} %get-tuple-element.37), channel_id=1, source_target_pairs={{0,1},{1,0},{2,3},{3,2},{4,5},{5,4},{6,7},{7,6}} | collective-permute-start | bytes 25165832 | tf_op jit(solution)/shard_map/ppermute | solution.py:243
  546.7 67.6 %collective-permute-start.6 = (f32[1024,2048]{1,0:T(8,128)}, f32[1024,2048]{1,0:T(8,128)}, u32[]{:S(2)}, u32[]{:S(2)}) collective-permute-start(f32[1024,2048]{1,0:T(8,128)} %get-tuple-element.39), channel_id=1, source_target_pairs={{0,1},{1,0},{2,3},{3,2},{4,5},{5,4},{6,7},{7,6}} | collective-permute-start | bytes 25165832 | tf_op jit(solution)/shard_map/ppermute | solution.py:243
  908.6 363.0 %collective-permute-start.9 = (f32[2048,2048]{1,0:T(8,128)}, f32[2048,2048]{1,0:T(8,128)}, u32[]{:S(2)}, u32[]{:S(2)}) collective-permute-start(f32[2048,2048]{1,0:T(8,128)} %get-tuple-element.43), channel_id=1, source_target_pairs={{0,1},{1,0},{2,3},{3,2},{4,5},{5,4},{6,7},{7,6}} | collective-permute-start | bytes 50331656 | tf_op jit(solution)/shard_map/ppermute | solution.py:250
  908.6 183.7 %collective-permute-start.1 = (f32[1024,2048]{1,0:T(8,128)}, f32[1024,2048]{1,0:T(8,128)}, u32[]{:S(2)}, u32[]{:S(2)}) collective-permute-start(f32[1024,2048]{1,0:T(8,128)} %fusion.3), channel_id=1, source_target_pairs={{0,4},{4,0},{1,5},{5,1},{2,6},{6,2},{3,7},{7,3}} | collective-permute-start | bytes 25165832 | tf_op jit(solution)/shard_map/ppermute | solution.py:248
  908.8 362.8 %collective-permute-start.7 = (f32[1024,2048]{1,0:T(8,128)}, f32[1024,2048]{1,0:T(8,128)}, u32[]{:S(2)}, u32[]{:S(2)}) collective-permute-start(f32[1024,2048]{1,0:T(8,128)} %fusion.4), channel_id=1, source_target_pairs={{0,4},{4,0},{1,5},{5,1},{2,6},{6,2},{3,7},{7,3}} | collective-permute-start | bytes 25165832 | tf_op jit(solution)/shard_map/ppermute | solution.py:248
  910.7 392.8 %collective-permute-start.10 = (f32[1024,2048]{1,0:T(8,128)}, f32[1024,2048]{1,0:T(8,128)}, u32[]{:S(2)}, u32[]{:S(2)}) collective-permute-start(f32[1024,2048]{1,0:T(8,128)} %add.195), channel_id=1, source_target_pairs={{0,2},{1,3},{2,0},{3,1},{4,6},{5,7},{6,4},{7,5}} | collective-permute-start | bytes 25165832 | tf_op jit(solution)/shard_map/ppermute | solution.py:247
  910.7 392.8 %collective-permute-start.11 = (f32[1024,2048]{1,0:T(8,128)}, f32[1024,2048]{1,0:T(8,128)}, u32[]{:S(2)}, u32[]{:S(2)}) collective-permute-start(f32[1024,2048]{1,0:T(8,128)} %add.196), channel_id=1, source_target_pairs={{0,2},{1,3},{2,0},{3,1},{4,6},{5,7},{6,4},{7,5}} | collective-permute-start | bytes 25165832 | tf_op jit(solution)/shard_map/ppermute | solution.py:247

commit v3 on v2

v3 whole, which is shorter than its diff:
```python
import functools

import jax
import jax.numpy as jnp
from jax import lax
from jax.experimental import pallas as pl
from jax.experimental.pallas import tpu as pltpu
from jax.sharding import PartitionSpec as P


CAP_FACTOR = 4
TILE = 256
UNROLL = 8
LENT = 2
PAIR = 2
LANES = 128


def capacity_rows(n_tok, top_k, n_exp):
    return min(n_tok, ((CAP_FACTOR * n_tok * top_k // n_exp + 7) // 8) * 8)


def token_of(copy_id, top_k):
    return lax.div(copy_id, top_k) if top_k & (top_k - 1) else lax.shift_right_logical(copy_id, top_k.bit_length() - 1)


def segment(offs, expert, start, q):
    base = offs[expert * (PAIR + 1) + q]
    lo = jnp.maximum(base, start)
    hi = jnp.minimum(offs[expert * (PAIR + 1) + q + 1], start + TILE)
    return lo - start, jnp.maximum(hi - lo, 0), lo - base


def weights(step, tile_exp, tile_row, groups, n_exps, n_own, pairs, sems):
    expert = tile_exp[step]
    slot = groups[expert] & 1

    def fetch(e, slot):
        for i, (own, lent, buf) in enumerate(pairs):

            @pl.when(e < n_own)
            def _():
                pltpu.make_async_copy(own.at[e], buf.at[slot], sems.at[i, slot]).start()

            @pl.when(e >= n_own)
            def _():
                pltpu.make_async_copy(lent.at[e - n_own], buf.at[slot], sems.at[i, slot]).start()

    @pl.when(step == 0)
    def _():
        fetch(expert, slot)

    @pl.when(tile_row[step] == 0)
    def _():
        following = groups[n_exps + expert]

        @pl.when(following < n_exps)
        def _():
            fetch(following, 1 - slot)

        for i, (own, _, buf) in enumerate(pairs):
            pltpu.make_async_copy(own.at[0], buf.at[slot], sems.at[i, slot]).wait()

    return slot


def up_kernel(n_tok, top_k, n_local, n_exps, table_cols, tile_exp, tile_row, offs, groups, owner, *refs):
    *parts, w1, w3, lent1, lent3, u_ref, tok_vmem, rows_vmem, w1_vmem, w3_vmem, sems, w_sems = refs
    step = pl.program_id(0)

    @pl.when(step == 0)
    def _():
        rows = PAIR * n_tok // len(parts)
        copies = [pltpu.make_async_copy(src, tok_vmem.at[pl.ds(i * rows, rows)], sems.at[i]) for i, src in enumerate(parts)]
        for copy in copies:
            copy.start()
        for copy in copies:
            copy.wait()

    @pl.when(step < tile_row[pl.num_programs(0)])
    def _():
        w_slot = weights(step, tile_exp, tile_row, groups, n_exps, n_local, ((w1, lent1, w1_vmem), (w3, lent3, w3_vmem)), w_sems)
        expert, start = tile_exp[step], tile_row[step]
        for q in range(PAIR):
            dst, count, slot = segment(offs, expert, start, q)
            src = (q * n_exps + expert) * table_cols + slot

            def gather(g, carry):
                rows = [tok_vmem[token_of(owner[src + g * UNROLL + j], top_k)] for j in range(UNROLL)]
                for j in range(UNROLL):
                    rows_vmem[dst + g * UNROLL + j] = rows[j]
                return carry

            lax.fori_loop(0, lax.div(count, UNROLL), gather, 0)

        rows = rows_vmem[...].reshape(TILE, -1)
        pre_gate = jnp.dot(rows, w1_vmem[w_slot], preferred_element_type=jnp.float32)
        pre_up = jnp.dot(rows, w3_vmem[w_slot], preferred_element_type=jnp.float32)
        u_ref[...] = (jax.nn.silu(pre_gate) * pre_up).astype(jnp.bfloat16)


def down_kernel(n_tok, top_k, n_local, n_exps, table_cols, tile_exp, tile_row, offs, groups, owner, gates, u_ref, w2, lent2, *refs):
    *outs, acc, tile_vmem, w2_vmem, sems, w_sems = refs
    step = pl.program_id(0)
    cols = w2.shape[2] // LANES

    @pl.when(step == 0)
    def _():
        def clear(g, carry):
            acc[pl.ds(g * 8, 8)] = jnp.zeros((8, cols, LANES), jnp.float32)
            return carry

        lax.fori_loop(0, PAIR * n_tok // 8, clear, 0)

    @pl.when(step < tile_row[pl.num_programs(0)])
    def _():
        w_slot = weights(step, tile_exp, tile_row, groups, n_exps, n_local, ((w2, lent2, w2_vmem),), w_sems)
        out = jnp.dot(u_ref[...], w2_vmem[w_slot], preferred_element_type=jnp.float32).astype(jnp.bfloat16).astype(jnp.float32)
        for b in range(TILE // 8):
            for c in range(cols):
                tile_vmem[pl.ds(b * 8 * cols + c, 8, stride=cols), :] = out[b * 8 : (b + 1) * 8, c * LANES : (c + 1) * LANES]

        expert, start = tile_exp[step], tile_row[step]
        for q in range(PAIR):
            dst, count, slot = segment(offs, expert, start, q)
            src = (q * n_exps + expert) * table_cols + slot

            def scatter(g, carry):
                copy_ids = [owner[src + g * UNROLL + j] for j in range(UNROLL)]
                toks = [token_of(copy_id, top_k) for copy_id in copy_ids]
                firsts = [pl.multiple_of((dst + g * UNROLL + j) * cols, cols) for j in range(UNROLL)]
                vals = [tile_vmem[pl.ds(firsts[j], cols), :] * gates[copy_ids[j]] for j in range(UNROLL)]
                olds = [acc[t] for t in toks]
                for j in range(UNROLL):
                    acc[toks[j]] = olds[j] + vals[j]
                return carry

            lax.fori_loop(0, lax.div(count, UNROLL), scatter, 0)

    @pl.when(step == pl.num_programs(0) - 1)
    def _():
        rows = PAIR * n_tok // len(outs)
        copies = [
            pltpu.make_async_copy(acc.at[pl.ds(i * rows, rows), c, :], dst.at[:, pl.ds(c * LANES, LANES)], sems.at[i * cols + c])
            for i, dst in enumerate(outs)
            for c in range(cols)
        ]
        for copy in copies:
            copy.start()
        for copy in copies:
            copy.wait()


def lend_kernel(ids, *refs):
    for i in range(3):
        refs[3 + i][...] = refs[i][...]


def solution(mesh):
    ep_size = mesh.shape["ep"]
    row_spec = P(("data", "ep", "tp"), None)
    expert_spec = P("ep", None, None)
    core_swap = [(r, r ^ 1) for r in range(ep_size)]
    chip_swap = [(r, r ^ 2) for r in range(ep_size)]

    def layer_body(tokens, expert_ids, gate_vals, slot_ids, send_counts, shared_w1, shared_w3, shared_w2, expert_w1, expert_w3, expert_w2):
        n_tok, d_model = tokens.shape
        top_k = expert_ids.shape[1]
        n_local, _, d_ff = expert_w1.shape
        n_exp = n_local * ep_size
        capacity = capacity_rows(n_tok, top_k, n_exp)
        table_cols = capacity + UNROLL
        max_tiles = (n_local + LENT) * PAIR * (capacity + UNROLL - 1) // TILE + n_local + LENT
        rank = lax.axis_index("ep")

        toks3 = tokens.reshape(n_tok, d_model // LANES, LANES)
        x_chip = lax.ppermute(toks3, "ep", chip_swap)
        peer_rows = [lax.ppermute(part, "tp", [(0, 1), (1, 0)]) for part in jnp.split(tokens, 2)]
        x_core = lax.ppermute(toks3, "ep", core_swap)
        x_diag = lax.ppermute(x_chip, "ep", core_swap)

        slots = jnp.where((slot_ids >= 0) & (slot_ids < capacity), slot_ids, table_cols)
        copy_ids = jnp.arange(n_tok * top_k, dtype=jnp.int32)
        dest = jnp.where(slots < capacity, expert_ids * table_cols + slots, n_exp * table_cols).reshape(-1)
        owner = jnp.zeros((n_exp * table_cols,), jnp.int32).at[dest].set(copy_ids, mode="drop").reshape(n_exp, table_cols)
        owner = jnp.concatenate([owner[:, :-1], send_counts[0][:, None]], axis=1).reshape(ep_size, n_local * table_cols)
        flat_gates = jnp.broadcast_to(gate_vals.reshape(1, -1), (ep_size, n_tok * top_k))
        swapped_owner = owner.reshape(ep_size // 2, 2, -1)[:, ::-1].reshape(ep_size, -1)
        message = jnp.concatenate([owner.astype(jnp.float32), swapped_owner.astype(jnp.float32), flat_gates], axis=1)
        message = lax.all_to_all(message, "ep", 0, 0, tiled=True)
        message = jnp.take(message, rank ^ jnp.arange(ep_size, dtype=jnp.int32), axis=0)
        chip_owner = message[:, : 2 * n_local * table_cols].astype(jnp.int32).reshape(ep_size, 2 * n_local, table_cols)
        gates = message[:, 2 * n_local * table_cols :]
        chip_counts = jnp.minimum(chip_owner[:, :, -1], capacity)

        def largest(loads):
            found = []
            for _ in range(LENT):
                found.append(jnp.argmax(loads).astype(jnp.int32))
                loads = jnp.where(jnp.arange(n_local) == found[-1], -1, loads)
            return jnp.stack(found)

        lent = largest(lax.dynamic_slice_in_dim(jnp.minimum(send_counts[0], capacity), rank * n_local, n_local))
        w_arrays = (expert_w1, expert_w3, expert_w2)
        lend_in = [pl.BlockSpec((1, w.shape[1] // 2, w.shape[2]), lambda i, j, ids: (ids[i], j, 0)) for w in w_arrays]
        lend_out = [pl.BlockSpec((1, w.shape[1] // 2, w.shape[2]), lambda i, j, ids: (i, j, 0)) for w in w_arrays]
        lent_w = pl.pallas_call(
            lend_kernel,
            grid_spec=pltpu.PrefetchScalarGridSpec(num_scalar_prefetch=1, grid=(LENT, 2), in_specs=lend_in, out_specs=lend_out),
            out_shape=[jax.ShapeDtypeStruct((LENT, *w.shape[1:]), w.dtype) for w in w_arrays],
            compiler_params=pltpu.CompilerParams(vmem_limit_bytes=60 * 2**20),
            cost_estimate=pl.CostEstimate(flops=10**9, bytes_accessed=12 * LENT * d_model * d_ff, transcendentals=0),
            name="lend",
        )(lent, *w_arrays)
        got1, got3, got2 = [lax.ppermute(w, "ep", core_swap) for w in lent_w]

        sizes = jnp.sum(chip_counts, axis=0)
        borrowed = largest(chip_counts[1, n_local:])
        tiles_of = (sizes + TILE - 1) // TILE
        diff = jnp.sum(tiles_of[:n_local]) - jnp.sum(tiles_of[n_local:])
        give, take = [], []
        gap = diff
        for i in range(LENT):
            give.append(gap > tiles_of[lent[i]])
            gap = jnp.where(give[-1], gap - 2 * tiles_of[lent[i]], gap)
        gap = -diff
        for i in range(LENT):
            take.append(gap > tiles_of[n_local + borrowed[i]])
            gap = jnp.where(take[-1], gap - 2 * tiles_of[n_local + borrowed[i]], gap)
        given = sum(((jnp.arange(n_local) == lent[i]) & give[i]).astype(jnp.int32) for i in range(LENT)) > 0
        owner = jnp.concatenate([chip_owner[:, :n_local]] + [lax.dynamic_slice_in_dim(chip_owner, n_local + borrowed[i], 1, axis=1) for i in range(LENT)], axis=1)
        counts = jnp.minimum(owner[:, :, -1], capacity)
        active = jnp.concatenate([~given, jnp.stack(take)])
        counts = jnp.where(active[None, :], counts, 0)
        n_exps = n_local + LENT

        any_spec = pl.BlockSpec(memory_space=pl.ANY)
        avg_rows = PAIR * n_tok * top_k // 2

        def plan(first):
            cnt = counts[first : first + PAIR]
            padded = (cnt + UNROLL - 1) // UNROLL * UNROLL
            offs = jnp.concatenate([jnp.zeros((1, n_exps), jnp.int32), jnp.cumsum(padded, axis=0, dtype=jnp.int32)], axis=0)
            tiles = (offs[-1] + TILE - 1) // TILE
            ends = jnp.cumsum(tiles, dtype=jnp.int32)
            last = jnp.maximum(ends[-1], 1) - 1
            ids = jnp.minimum(jnp.arange(max_tiles, dtype=jnp.int32), last)
            past = ids[:, None] >= ends[None, :]
            tile_exp = jnp.minimum(jnp.sum(past, axis=1, dtype=jnp.int32), n_exps - 1)
            tile_row = jnp.append((ids - jnp.sum(jnp.where(past, tiles[None, :], 0), axis=1, dtype=jnp.int32)) * TILE, last + 1)
            used = tiles > 0
            exps = jnp.arange(n_exps, dtype=jnp.int32)
            later = (exps[None, :] > exps[:, None]) & used[None, :]
            following = jnp.min(jnp.where(later, exps[None, :], n_exps), axis=1)
            groups = jnp.append(jnp.cumsum(used, dtype=jnp.int32), following)
            col = jnp.arange(table_cols, dtype=jnp.int32)
            base = jnp.arange(PAIR, dtype=jnp.int32)[:, None, None] * (n_tok * top_k)
            spare = PAIR * n_tok * top_k + (col % UNROLL) * top_k
            rows = jnp.where(col < cnt[:, :, None], owner[first : first + PAIR] + base, spare).reshape(-1)
            gate = jnp.append(gates[first : first + PAIR].reshape(-1), jnp.zeros((UNROLL * top_k,), jnp.float32))
            return tile_exp, tile_row, offs.T.reshape(-1), groups, rows, gate

        def experts(planned, parts, n_out):
            tile_exp, tile_row, offs, groups, rows, gate = planned
            hidden = pl.pallas_call(
                functools.partial(up_kernel, n_tok, top_k, n_local, n_exps, table_cols),
                grid_spec=pltpu.PrefetchScalarGridSpec(
                    num_scalar_prefetch=5,
                    grid=(max_tiles,),
                    in_specs=[any_spec] * (len(parts) + 4),
                    out_specs=pl.BlockSpec((TILE, d_ff), lambda i, te, tr, of, gr, ow: (jnp.minimum(i, tr[max_tiles] - 1), 0)),
                    scratch_shapes=[
                        pltpu.VMEM((PAIR * n_tok + UNROLL, d_model // LANES, LANES), jnp.bfloat16),
                        pltpu.VMEM((TILE, d_model // LANES, LANES), jnp.bfloat16),
                        pltpu.VMEM((2, d_model, d_ff), jnp.bfloat16),
                        pltpu.VMEM((2, d_model, d_ff), jnp.bfloat16),
                        pltpu.SemaphoreType.DMA((len(parts),)),
                        pltpu.SemaphoreType.DMA((2, 2)),
                    ],
                ),
                out_shape=jax.ShapeDtypeStruct((max_tiles * TILE, d_ff), jnp.bfloat16),
                compiler_params=pltpu.CompilerParams(vmem_limit_bytes=60 * 2**20, dimension_semantics=("arbitrary",)),
                cost_estimate=pl.CostEstimate(flops=4 * avg_rows * d_model * d_ff, bytes_accessed=4 * n_local * d_model * d_ff, transcendentals=0),
                name="expert_up",
            )(tile_exp, tile_row, offs, groups, rows, *parts, expert_w1, expert_w3, got1, got3)
            return pl.pallas_call(
                functools.partial(down_kernel, n_tok, top_k, n_local, n_exps, table_cols),
                grid_spec=pltpu.PrefetchScalarGridSpec(
                    num_scalar_prefetch=6,
                    grid=(max_tiles,),
                    in_specs=[
                        pl.BlockSpec((TILE, d_ff), lambda i, te, tr, of, gr, ow, ga: (jnp.minimum(i, tr[max_tiles] - 1), 0)),
                        any_spec,
                        any_spec,
                    ],
                    out_specs=[any_spec] * n_out,
                    scratch_shapes=[
                        pltpu.VMEM((PAIR * n_tok + UNROLL, d_model // LANES, LANES), jnp.float32),
                        pltpu.VMEM((TILE * d_model // LANES, LANES), jnp.float32),
                        pltpu.VMEM((2, d_ff, d_model), jnp.bfloat16),
                        pltpu.SemaphoreType.DMA((n_out * d_model // LANES,)),
                        pltpu.SemaphoreType.DMA((1, 2)),
                    ],
                ),
                out_shape=[jax.ShapeDtypeStruct((PAIR * n_tok // n_out, d_model), jnp.float32)] * n_out,
                compiler_params=pltpu.CompilerParams(vmem_limit_bytes=60 * 2**20, dimension_semantics=("arbitrary",)),
                cost_estimate=pl.CostEstimate(flops=2 * avg_rows * d_model * d_ff, bytes_accessed=2 * n_local * d_model * d_ff, transcendentals=0),
                name="expert_down",
            )(tile_exp, tile_row, offs, groups, rows, gate, hidden, expert_w2, got2)

        def shared_part(rows):
            pre_gate = jnp.dot(rows, shared_w1, preferred_element_type=jnp.float32)
            pre_up = jnp.dot(rows, shared_w3, preferred_element_type=jnp.float32)
            shared_hidden = (jax.nn.silu(pre_gate) * pre_up).astype(jnp.bfloat16)
            return jnp.dot(shared_hidden, shared_w2, preferred_element_type=jnp.float32)

        far_plan, near_plan = plan(PAIR), plan(0)
        own_part = shared_part(tokens)
        peer_rows[0], own_part = lax.optimization_barrier((peer_rows[0], own_part))
        peer_0 = shared_part(peer_rows[0])
        tile_exp, peer_0 = lax.optimization_barrier((far_plan[0], peer_0))
        far_sums = experts((tile_exp, *far_plan[1:]), (x_chip, x_diag), 4)
        peer_rows[1], *far_sums = lax.optimization_barrier((peer_rows[1], *far_sums))
        swapped = [lax.ppermute(part, "ep", core_swap) for part in far_sums[2:]]
        chip_sums = [mine + theirs for mine, theirs in zip(far_sums[:2], swapped)]
        peer_1 = shared_part(peer_rows[1])
        tile_exp, peer_1, *chip_sums = lax.optimization_barrier((near_plan[0], peer_1, *chip_sums))
        back = [lax.ppermute(part, "ep", chip_swap) for part in chip_sums]
        peer_back = [lax.ppermute(part, "tp", [(0, 1), (1, 0)]) for part in (peer_0, peer_1)]
        own, core = experts((tile_exp, *near_plan[1:]), (toks3, x_core), 2)
        near = own + lax.ppermute(core, "ep", core_swap)
        kept = tokens.astype(jnp.float32) + own_part + jnp.concatenate(peer_back) + near
        kept, *back = lax.optimization_barrier((kept, *back))
        return (kept + jnp.concatenate(back)).astype(jnp.bfloat16)

    return jax.shard_map(
        layer_body,
        mesh=mesh,
        in_specs=(row_spec, row_spec, row_spec, row_spec, row_spec, P(None, "tp"), P(None, "tp"), P("tp", None), expert_spec, expert_spec, expert_spec),
        out_specs=row_spec,
        check_vma=False,
    )
```

time: 1320 us -> 1210 us (0.917)
  the two profiles are of different devices: /device:TPU:6 before, /device:TPU:2 now
where the time goes in v3:
time: 1210 us; the launch traced here: 1200 us
  Pallas kernels  397 us (33%)
  waiting for transfers between devices  363 us (30%)
  matrix products  209 us (17%)
  other arithmetic  85.7 us (7%)
  starting transfers between devices  70.2 us (6%)
  local copies, waits for them, and re-layouts  61.5 us (5%)
  between operations  13.6 us (1%)
    ppermute x4, waiting for transfers between devices, layer_body(): lax.ppermute(part, 'tp', [(0, 1), (1, 0)])  358 us
    pallas_call x2, Pallas kernels, experts(): pl.pallas_call(functools.partial(up_kernel, n_tok, top_k, n_local, n_exps...  205 us
    pallas_call x2, Pallas kernels, experts(): pl.pallas_call(functools.partial(down_kernel, n_tok, top_k, n_local, n_ex...  169 us
    dot_general x3, matrix products, shared_part(): return jnp.dot(shared_hidden, shared_w2, preferred_element_type=jnp.float32)  105 us
    dot_general x3, matrix products, shared_part(): pre_gate = jnp.dot(rows, shared_w1, preferred_element_type=jnp.float32)  69.3 us
    dot_general x1, matrix products, shared_part(): pre_up = jnp.dot(rows, shared_w3, preferred_element_type=jnp.float32)  34.4 us
    add x1, other arithmetic, layer_body(): tokens.astype(jnp.float32) + own_part + jnp.concatenate(peer_back) + near  31.7 us
    scatter x1, local copies, waits for them, and re-layouts, layer_body(): jnp.zeros((n_exp * table_cols,), jnp.int32).at[dest]  30.5 us
  transfers between devices with their start and end apart: 16, of which 3 were waited for; matrix products, arithmetic and copies ran while one was open for 27% of the time, Pallas kernels for 18%

profile of v3, /device:TPU:2, one launch (start us, length us, event | category | flops | bytes accessed | tf_op | source)
XLA Modules:
  0.0 1199.8 jit_solution(9367139496559435747)
XLA Ops:
  0.0 9.8 copy.61
  11.1 30.5 %scatter_custom_fusion = s32[33600]{0:T(1024)S(1)} fusion(s32[8192]{0:T(1024)S(1)} %bitcast.96, s32[8192]{0:T(1024)S(1)} %iota.71, s32[]{:T(128)} %constant.161.clone.1), kind=kCustom, calls=%fused_computation.24 | custom fusion | bytes 134404 | tf_op jit(solution)/shard_map/scatter | solution.py:185
  42.1 1.8 rev.3
  46.8 6.3 all-to-all-start
  53.1 6.1 fusion.34
  59.2 1.5 collective-permute-start
  62.9 1.9 pad_add_fusion.5.ids
  64.8 23.2 %lend.1 = (bf16[2,2048,1408]{2,1,0:T(8,128)(2,1)}, bf16[2,2048,1408]{2,1,0:T(8,128)(2,1)}, bf16[2,1408,2048]{2,1,0:T(8,128)(2,1)}) custom-call(s32[2]{0:T(128)} %pad_add_fusion.5.ids, bf16[15,2048,1408]{2,1,0:T(8,128)(2,1)} %refs_2_.5, bf16[15,2048,1408]{2,1,0:T(8,128)(2,1)} %refs_3_.3, bf16[15,1408,2048]{2,1,0:T(8,128)(2,1)} %w2.3), custom_call_target="tpu_custom_call" | custom-call | flops 1000000000 | bytes 69206016 | tf_op jit(solution)/shard_map/lend/pallas_call | solution.py:207
  92.1 31.9 %fusion.41 = f32[2048,2816]{1,0:T(8,128)} fusion(bf16[2048,2048]{1,0:T(8,128)(2,1)} %param.11, bf16[2048,2816]{1,0:T(8,128)(2,1)} %param.16), kind=kOutput, calls=%fused_computation.139 | convolution fusion | flops 23622320128 | bytes 42991616 | tf_op jit(solution)/shard_map/dot_general | solution.py:312
  125.3 34.4 %multiply_convert_fusion.clone.4 = bf16[2048,2816]{1,0:T(8,128)(2,1)} fusion(f32[2048,2816]{1,0:T(8,128)} %fusion.41, bf16[2048,2048]{1,0:T(8,128)(2,1)} %param.11, bf16[2048,2816]{1,0:T(8,128)(2,1)} %param.17), kind=kOutput, calls=%fused_computation.2.clone.clone.clone.1 | convolution fusion | flops 23656923136 | bytes 54525952 | tf_op jit(solution)/shard_map/dot_general | solution.py:313
  159.7 32.3 %fusion.2 = f32[2048,2048]{1,0:T(8,128)} fusion(bf16[2816,2048]{1,0:T(8,128)(2,1)} %param.18, bf16[2048,2816]{1,0:T(8,128)(2,1)} %multiply_convert_fusion.clone.4), kind=kOutput, calls=%fused_computation.9 | convolution fusion | flops 23622320128 | bytes 39845888 | tf_op jit(solution)/shard_map/dot_general | solution.py:315
  192.0 4.7 all-to-all-done
  200.1 1.4 fusion.28
  225.2 18.7 %fusion.42 = f32[1024,2816]{1,0:T(8,128)} fusion(bf16[1024,2048]{1,0:T(8,128)(2,1)} %collective-permute-done, bf16[2048,2816]{1,0:T(8,128)(2,1)} %param.16), kind=kOutput, calls=%fused_computation.140 | convolution fusion | flops 11811160064 | bytes 27262976 | tf_op jit(solution)/shard_map/dot_general | solution.py:312
  243.9 36.4 %fusion.3 = f32[1024,2048]{1,0:T(8,128)} fusion(bf16[2816,2048]{1,0:T(8,128)(2,1)} %param.18, f32[1024,2816]{1,0:T(8,128)} %fusion.42, bf16[1024,2048]{1,0:T(8,128)(2,1)} %collective-permute-done, bf16[2048,2816]{1,0:T(8,128)(2,1)} %param.17), kind=kOutput, calls=%fused_computation.10 | convolution fusion | flops 23639621632 | bytes 47185920 | tf_op jit(solution)/shard_map/dot_general | solution.py:315
  280.3 1.5 collective-permute-start.2
  281.8 102.3 %expert_up.2.u_ref = bf16[23296,1408]{1,0:T(8,128)(2,1)} custom-call(s32[91]{0:T(128)} %broadcast_minimum_fusion.1.tile_exp, s32[92]{0:T(128)} %pad_add_fusion.3.tile_row, s32[51]{0:T(128)} %reshape.317.offs, s32[34]{0:T(128)} %pad_add_fusion.4.groups, s32[19040]{0:T(1024)} %reshape.319.owner, bf16[2048,16,128]{2,1,0:T(8,128)(2,1)} %collective-permute-done.3.refs_0_, ...), custom_call_target="tpu_custom_call" | custom-call | flops 94489280512 | bytes 173015040 | tf_op jit(solution)/shard_map/expert_up/pallas_call | solution.py:265
  384.2 84.6 %expert_down.2 = (f32[1024,2048]{1,0:T(8,128)}, f32[1024,2048]{1,0:T(8,128)}, f32[1024,2048]{1,0:T(8,128)}, f32[1024,2048]{1,0:T(8,128)}) custom-call(s32[91]{0:T(128)} %broadcast_minimum_fusion.1.tile_exp, s32[92]{0:T(128)} %pad_add_fusion.3.tile_row, s32[51]{0:T(128)} %reshape.317.offs, s32[34]{0:T(128)} %pad_add_fusion.4.groups, s32[19040]{0:T(1024)} %reshape.319.owner, ...), custom_call_target="tpu_custom_call" | custom-call | flops 47244640256 | bytes 86507520 | tf_op jit(solution)/shard_map/expert_down/pallas_call | solution.py:286
  468.8 27.6 %collective-permute-start.9 = (f32[1024,2048]{1,0:T(8,128)}, f32[1024,2048]{1,0:T(8,128)}, u32[]{:S(2)}, u32[]{:S(2)}) collective-permute-start(f32[1024,2048]{1,0:T(8,128)} %get-tuple-element.53), channel_id=1, source_target_pairs={{0,1},{1,0},{2,3},{3,2},{4,5},{5,4},{6,7},{7,6}} | collective-permute-start | bytes 25165832 | tf_op jit(solution)/shard_map/ppermute | solution.py:324
  496.5 18.7 %fusion.43 = f32[1024,2816]{1,0:T(8,128)} fusion(bf16[1024,2048]{1,0:T(8,128)(2,1)} %collective-permute-done.2, bf16[2048,2816]{1,0:T(8,128)(2,1)} %param.16), kind=kOutput, calls=%fused_computation.141 | convolution fusion | flops 11811160064 | bytes 27262976 | tf_op jit(solution)/shard_map/dot_general | solution.py:312
  515.1 36.4 %fusion.4 = f32[1024,2048]{1,0:T(8,128)} fusion(bf16[2816,2048]{1,0:T(8,128)(2,1)} %param.18, f32[1024,2816]{1,0:T(8,128)} %fusion.43, bf16[1024,2048]{1,0:T(8,128)(2,1)} %collective-permute-done.2, bf16[2048,2816]{1,0:T(8,128)(2,1)} %param.17), kind=kOutput, calls=%fused_computation.11 | convolution fusion | flops 23639621632 | bytes 47185920 | tf_op jit(solution)/shard_map/dot_general | solution.py:315
  551.6 11.8 add.261
  563.4 11.7 add.260
  575.1 102.5 %expert_up.3.u_ref = bf16[23296,1408]{1,0:T(8,128)(2,1)} custom-call(s32[91]{0:T(128)} %broadcast_minimum_fusion.tile_exp, s32[92]{0:T(128)} %pad_add_fusion.6.tile_row, s32[51]{0:T(128)} %reshape.323.offs, s32[34]{0:T(128)} %pad_add_fusion.7.groups, s32[19040]{0:T(1024)} %reshape.325.owner, bf16[2048,16,128]{2,1,0:T(8,128)(2,1)} %bitcast.92, ...), custom_call_target="tpu_custom_call" | custom-call | flops 94489280512 | bytes 173015040 | tf_op jit(solution)/shard_map/expert_up/pallas_call | solution.py:265
  677.6 84.1 %expert_down.3 = (f32[2048,2048]{1,0:T(8,128)}, f32[2048,2048]{1,0:T(8,128)}) custom-call(s32[91]{0:T(128)} %broadcast_minimum_fusion.tile_exp, s32[92]{0:T(128)} %pad_add_fusion.6.tile_row, s32[51]{0:T(128)} %reshape.323.offs, s32[34]{0:T(128)} %pad_add_fusion.7.groups, s32[19040]{0:T(1024)} %reshape.325.owner, f32[16416]{0:T(1024)} %concatenate.57.gates, ...), custom_call_target="tpu_custom_call" | custom-call | flops 47244640256 | bytes 86507520 | tf_op jit(solution)/shard_map/expert_down/pallas_call | solution.py:286
  761.7 28.2 %collective-permute-start.12 = (f32[2048,2048]{1,0:T(8,128)}, f32[2048,2048]{1,0:T(8,128)}, u32[]{:S(2)}, u32[]{:S(2)}) collective-permute-start(f32[2048,2048]{1,0:T(8,128)} %get-tuple-element.57), channel_id=1, source_target_pairs={{0,1},{1,0},{2,3},{3,2},{4,5},{5,4},{6,7},{7,6}} | collective-permute-start | bytes 50331656 | tf_op jit(solution)/shard_map/ppermute | solution.py:331
  790.3 1.6 collective-permute-start.10
  791.9 2.0 collective-permute-start.14
  793.9 179.6 %collective-permute-done.1 = f32[1024,2048]{1,0:T(8,128)} collective-permute-done((f32[1024,2048]{1,0:T(8,128)}, f32[1024,2048]{1,0:T(8,128)}, u32[]{:S(2)}, u32[]{:S(2)}) %collective-permute-start.1) | collective-permute-done | bytes 8388640 | tf_op jit(solution)/shard_map/ppermute | solution.py:329
  973.5 178.8 %collective-permute-done.10 = f32[1024,2048]{1,0:T(8,128)} collective-permute-done((f32[1024,2048]{1,0:T(8,128)}, f32[1024,2048]{1,0:T(8,128)}, u32[]{:S(2)}, u32[]{:S(2)}) %collective-permute-start.10) | collective-permute-done | bytes 8388640 | tf_op jit(solution)/shard_map/ppermute | solution.py:329
  1152.4 31.7 %fusion = f32[2048,2048]{1,0:T(8,128)} fusion(f32[1024,2048]{1,0:T(8,128)} %collective-permute-done.10, f32[1024,2048]{1,0:T(8,128)} %collective-permute-done.1, f32[2048,2048]{1,0:T(8,128)} %get-tuple-element.56, f32[2048,2048]{1,0:T(8,128)} %collective-permute-done.12, f32[2048,2048]{1,0:T(8,128)} %fusion.2, bf16[2048,2048]{1,0:T(8,128)(2,1)} %param.11), kind=kLoop, calls=%fused_computation.4 | loop fusion | flops 25165824 | bytes 92274688 | tf_op jit(solution)/shard_map/add | solution.py:332
  1184.1 15.3 %fusion.1 = bf16[2048,2048]{1,0:T(8,128)(2,1)} fusion(f32[2048,2048]{1,0:T(8,128)} %fusion, f32[1024,2048]{1,0:T(8,128)} %collective-permute-done.14, f32[1024,2048]{1,0:T(8,128)} %collective-permute-done.13), kind=kLoop, calls=%fused_computation.6 | loop fusion | flops 12582912 | bytes 41943040 | tf_op jit(solution)/shard_map/convert_element_type | solution.py:334
  (123 shorter events, 26.7 us)
Async XLA Ops:
  0.0 9.9 copy-start
  0.0 9.9 copy-start.1
  0.0 41.7 %copy-start.3 = (s32[1,60]{1,0:T(1,128)S(1)}, s32[1,60]{1,0:T(1,128)}, u32[]{:S(2)}) copy-start(s32[1,60]{1,0:T(1,128)} %param.15) | copy-start | bytes 724
  0.0 44.2 %copy-start.2 = (f32[2048,4]{0,1:T(4,128)S(1)}, f32[2048,4]{0,1:T(4,128)}, u32[]{:S(2)}) copy-start(f32[2048,4]{0,1:T(4,128)} %param.13) | copy-start | bytes 98308
  9.9 214.8 %collective-permute-start.3 = (bf16[2048,16,128]{2,1,0:T(8,128)(2,1)}, bf16[2048,16,128]{2,1,0:T(8,128)(2,1)}, u32[]{:S(2)}, u32[]{:S(2)}) collective-permute-start(bf16[2048,16,128]{2,1,0:T(8,128)(2,1)} %bitcast.90), channel_id=1, source_target_pairs={{0,2},{1,3},{2,0},{3,1},{4,6},{5,7},{6,4},{7,5}} | collective-permute-start | bytes 25165832 | tf_op jit(solution)/shard_map/ppermute | solution.py:177
  9.9 565.2 %collective-permute-start.11 = (bf16[2048,16,128]{2,1,0:T(8,128)(2,1)}, bf16[2048,16,128]{2,1,0:T(8,128)(2,1)}, u32[]{:S(2)}, u32[]{:S(2)}) collective-permute-start(bf16[2048,16,128]{2,1,0:T(8,128)(2,1)} %bitcast.91), channel_id=1, source_target_pairs={{0,1},{1,0},{2,3},{3,2},{4,5},{5,4},{6,7},{7,6}} | collective-permute-start | bytes 25165832 | tf_op jit(solution)/shard_map/ppermute | solution.py:179
  46.8 149.9 %all-to-all-start = ((f32[4,1,24992]{2,1,0:T(1,128)}), f32[4,1,24992]{2,1,0:T(1,128)}, u32[]{:S(2)}, u32[]{:S(2)}) async-start(f32[4,1,24992]{2,1,0:T(1,128)} %all_to_all.8), calls=%async_computation | async-start | bytes 802816 | tf_op jit(solution)/shard_map/all_to_all | solution.py:190
  59.2 165.4 %collective-permute-start = (bf16[1024,2048]{1,0:T(8,128)(2,1)}, bf16[1024,2048]{1,0:T(8,128)(2,1)}, u32[]{:S(2)}, u32[]{:S(2)}) collective-permute-start(bf16[1024,2048]{1,0:T(8,128)(2,1)} %get-tuple-element.81), channel_id=1, source_target_pairs={{0,4},{4,0},{1,5},{5,1},{2,6},{6,2},{3,7},{7,3}} | collective-permute-start | bytes 12582920 | tf_op jit(solution)/shard_map/ppermute | solution.py:178
  88.0 192.3 %collective-permute-start.5 = (bf16[2,2048,1408]{2,1,0:T(8,128)(2,1)}, bf16[2,2048,1408]{2,1,0:T(8,128)(2,1)}, u32[]{:S(2)}, u32[]{:S(2)}) collective-permute-start(bf16[2,2048,1408]{2,1,0:T(8,128)(2,1)} %get-tuple-element.42), channel_id=1, source_target_pairs={{0,1},{1,0},{2,3},{3,2},{4,5},{5,4},{6,7},{7,6}} | collective-permute-start | bytes 34603016 | tf_op jit(solution)/shard_map/ppermute | solution.py:215
  88.0 193.8 %collective-permute-start.6 = (bf16[2,2048,1408]{2,1,0:T(8,128)(2,1)}, bf16[2,2048,1408]{2,1,0:T(8,128)(2,1)}, u32[]{:S(2)}, u32[]{:S(2)}) collective-permute-start(bf16[2,2048,1408]{2,1,0:T(8,128)(2,1)} %get-tuple-element.43), channel_id=1, source_target_pairs={{0,1},{1,0},{2,3},{3,2},{4,5},{5,4},{6,7},{7,6}} | collective-permute-start | bytes 34603016 | tf_op jit(solution)/shard_map/ppermute | solution.py:215
  159.6 32.3 %copy-start.4 = (s32[4]{0:T(128)S(1)}, s32[4]{0:T(128)}, u32[]{:S(2)}) copy-start(s32[4]{0:T(128)} %fusion.29) | copy-start | bytes 52
  159.6 38.9 %copy-start.5 = (pred[4]{0:T(512)(128)(4,1)S(1)}, pred[4]{0:T(512)(128)(4,1)}, u32[]{:S(2)}) copy-start(pred[4]{0:T(512)(128)(4,1)} %compare_and_fusion) | copy-start | bytes 16
  224.6 159.5 %collective-permute-start.7 = (bf16[2,1408,2048]{2,1,0:T(8,128)(2,1)}, bf16[2,1408,2048]{2,1,0:T(8,128)(2,1)}, u32[]{:S(2)}, u32[]{:S(2)}) collective-permute-start(bf16[2,1408,2048]{2,1,0:T(8,128)(2,1)} %get-tuple-element.44), channel_id=1, source_target_pairs={{0,1},{1,0},{2,3},{3,2},{4,5},{5,4},{6,7},{7,6}} | collective-permute-start | bytes 34603016 | tf_op jit(solution)/shard_map/ppermute | solution.py:215
  224.7 57.2 %collective-permute-start.4 = (bf16[2048,16,128]{2,1,0:T(8,128)(2,1)}, bf16[2048,16,128]{2,1,0:T(8,128)(2,1)}, u32[]{:S(2)}, u32[]{:S(2)}) collective-permute-start(bf16[2048,16,128]{2,1,0:T(8,128)(2,1)} %collective-permute-done.3.refs_0_), channel_id=1, source_target_pairs={{0,1},{1,0},{2,3},{3,2},{4,5},{5,4},{6,7},{7,6}} | collective-permute-start | bytes 25165832 | tf_op jit(solution)/shard_map/ppermute | solution.py:180
  280.3 188.5 %collective-permute-start.2 = (bf16[1024,2048]{1,0:T(8,128)(2,1)}, bf16[1024,2048]{1,0:T(8,128)(2,1)}, u32[]{:S(2)}, u32[]{:S(2)}) collective-permute-start(bf16[1024,2048]{1,0:T(8,128)(2,1)} %get-tuple-element.82), channel_id=1, source_target_pairs={{0,4},{4,0},{1,5},{5,1},{2,6},{6,2},{3,7},{7,3}} | collective-permute-start | bytes 12582920 | tf_op jit(solution)/shard_map/ppermute | solution.py:178
  468.8 82.7 %collective-permute-start.9 = (f32[1024,2048]{1,0:T(8,128)}, f32[1024,2048]{1,0:T(8,128)}, u32[]{:S(2)}, u32[]{:S(2)}) collective-permute-start(f32[1024,2048]{1,0:T(8,128)} %get-tuple-element.53), channel_id=1, source_target_pairs={{0,1},{1,0},{2,3},{3,2},{4,5},{5,4},{6,7},{7,6}} | collective-permute-start | bytes 25165832 | tf_op jit(solution)/shard_map/ppermute | solution.py:324
  496.4 66.9 %collective-permute-start.8 = (f32[1024,2048]{1,0:T(8,128)}, f32[1024,2048]{1,0:T(8,128)}, u32[]{:S(2)}, u32[]{:S(2)}) collective-permute-start(f32[1024,2048]{1,0:T(8,128)} %get-tuple-element.51), channel_id=1, source_target_pairs={{0,1},{1,0},{2,3},{3,2},{4,5},{5,4},{6,7},{7,6}} | collective-permute-start | bytes 25165832 | tf_op jit(solution)/shard_map/ppermute | solution.py:324
  761.7 390.7 %collective-permute-start.12 = (f32[2048,2048]{1,0:T(8,128)}, f32[2048,2048]{1,0:T(8,128)}, u32[]{:S(2)}, u32[]{:S(2)}) collective-permute-start(f32[2048,2048]{1,0:T(8,128)} %get-tuple-element.57), channel_id=1, source_target_pairs={{0,1},{1,0},{2,3},{3,2},{4,5},{5,4},{6,7},{7,6}} | collective-permute-start | bytes 50331656 | tf_op jit(solution)/shard_map/ppermute | solution.py:331
  789.9 183.6 %collective-permute-start.1 = (f32[1024,2048]{1,0:T(8,128)}, f32[1024,2048]{1,0:T(8,128)}, u32[]{:S(2)}, u32[]{:S(2)}) collective-permute-start(f32[1024,2048]{1,0:T(8,128)} %fusion.3), channel_id=1, source_target_pairs={{0,4},{4,0},{1,5},{5,1},{2,6},{6,2},{3,7},{7,3}} | collective-permute-start | bytes 25165832 | tf_op jit(solution)/shard_map/ppermute | solution.py:329
  790.3 362.0 %collective-permute-start.10 = (f32[1024,2048]{1,0:T(8,128)}, f32[1024,2048]{1,0:T(8,128)}, u32[]{:S(2)}, u32[]{:S(2)}) collective-permute-start(f32[1024,2048]{1,0:T(8,128)} %fusion.4), channel_id=1, source_target_pairs={{0,4},{4,0},{1,5},{5,1},{2,6},{6,2},{3,7},{7,3}} | collective-permute-start | bytes 25165832 | tf_op jit(solution)/shard_map/ppermute | solution.py:329
  791.9 392.1 %collective-permute-start.13 = (f32[1024,2048]{1,0:T(8,128)}, f32[1024,2048]{1,0:T(8,128)}, u32[]{:S(2)}, u32[]{:S(2)}) collective-permute-start(f32[1024,2048]{1,0:T(8,128)} %add.260), channel_id=1, source_target_pairs={{0,2},{1,3},{2,0},{3,1},{4,6},{5,7},{6,4},{7,5}} | collective-permute-start | bytes 25165832 | tf_op jit(solution)/shard_map/ppermute | solution.py:328
  791.9 392.1 %collective-permute-start.14 = (f32[1024,2048]{1,0:T(8,128)}, f32[1024,2048]{1,0:T(8,128)}, u32[]{:S(2)}, u32[]{:S(2)}) collective-permute-start(f32[1024,2048]{1,0:T(8,128)} %add.261), channel_id=1, source_target_pairs={{0,2},{1,3},{2,0},{3,1},{4,6},{5,7},{6,4},{7,5}} | collective-permute-start | bytes 25165832 | tf_op jit(solution)/shard_map/ppermute | solution.py:328

commit v4 on v3

--- a/solution.py
+++ b/solution.py
@@ -11,7 +11,7 @@
 CAP_FACTOR = 4
 TILE = 256
 UNROLL = 8
-LENT = 2
+LENT = 3
 PAIR = 2
 LANES = 128
 
@@ -170,7 +170,7 @@
         n_exp = n_local * ep_size
         capacity = capacity_rows(n_tok, top_k, n_exp)
         table_cols = capacity + UNROLL
-        max_tiles = (n_local + LENT) * PAIR * (capacity + UNROLL - 1) // TILE + n_local + LENT
+        max_tiles = (PAIR * n_tok * top_k + (n_local + LENT) * PAIR * (UNROLL - 1)) // TILE + n_local + LENT
         rank = lax.axis_index("ep")
 
         toks3 = tokens.reshape(n_tok, d_model // LANES, LANES)
@@ -324,14 +324,13 @@
         swapped = [lax.ppermute(part, "ep", core_swap) for part in far_sums[2:]]
         chip_sums = [mine + theirs for mine, theirs in zip(far_sums[:2], swapped)]
         peer_1 = shared_part(peer_rows[1])
-        tile_exp, peer_1, *chip_sums = lax.optimization_barrier((near_plan[0], peer_1, *chip_sums))
+        tile_exp, peer_1 = lax.optimization_barrier((near_plan[0], peer_1))
         back = [lax.ppermute(part, "ep", chip_swap) for part in chip_sums]
         peer_back = [lax.ppermute(part, "tp", [(0, 1), (1, 0)]) for part in (peer_0, peer_1)]
         own, core = experts((tile_exp, *near_plan[1:]), (toks3, x_core), 2)
-        near = own + lax.ppermute(core, "ep", core_swap)
-        kept = tokens.astype(jnp.float32) + own_part + jnp.concatenate(peer_back) + near
-        kept, *back = lax.optimization_barrier((kept, *back))
-        return (kept + jnp.concatenate(back)).astype(jnp.bfloat16)
+        core = lax.ppermute(core, "ep", core_swap)
+        kept = lax.optimization_barrier(tokens.astype(jnp.float32) + own_part + jnp.concatenate(peer_back) + own)
+        return (kept + core + jnp.concatenate(back)).astype(jnp.bfloat16)
 
     return jax.shard_map(
         layer_body,

time: 1210 us -> 1200 us (level)
  the two profiles are of different devices: /device:TPU:2 before, /device:TPU:0 now
where the time goes in v4:
time: 1200 us; the launch traced here: 1180 us
  Pallas kernels  395 us (33%)
  waiting for transfers between devices  322 us (27%)
  matrix products  209 us (17%)
  other arithmetic  88.5 us (7%)
  starting transfers between devices  82.7 us (7%)
  local copies, waits for them, and re-layouts  61.8 us (5%)
  between operations  18.9 us (2%)
    ppermute x4, waiting for transfers between devices, layer_body(): lax.ppermute(part, 'tp', [(0, 1), (1, 0)])  294 us
    pallas_call x2, Pallas kernels, experts(): pl.pallas_call(functools.partial(up_kernel, n_tok, top_k, n_local, n_exps...  198 us
    pallas_call x2, Pallas kernels, experts(): pl.pallas_call(functools.partial(down_kernel, n_tok, top_k, n_local, n_ex...  163 us
    dot_general x3, matrix products, shared_part(): return jnp.dot(shared_hidden, shared_w2, preferred_element_type=jnp.float32)  105 us
    dot_general x3, matrix products, shared_part(): pre_gate = jnp.dot(rows, shared_w1, preferred_element_type=jnp.float32)  69.3 us
    ppermute x2, starting transfers between devices, layer_body(): back = [lax.ppermute(part, 'ep', chip_swap) for part in chip_sums]  42.9 us
    dot_general x1, matrix products, shared_part(): pre_up = jnp.dot(rows, shared_w3, preferred_element_type=jnp.float32)  34.4 us
    pallas_call x1, Pallas kernels, layer_body(): pl.pallas_call(lend_kernel, grid_spec=pltpu.PrefetchScalarGridSpec(num_sc...  34.3 us
  transfers between devices with their start and end apart: 16, of which 3 were waited for; matrix products, arithmetic and copies ran while one was open for 28% of the time, Pallas kernels for 34%

profile of v4, /device:TPU:0, one launch (start us, length us, event | category | flops | bytes accessed | tf_op | source)
XLA Modules:
  0.0 1177.1 jit_solution(297561030848895352)
XLA Ops:
  0.0 10.0 copy.62
  10.0 3.3 collective-permute-start.3
  14.6 30.5 %scatter_custom_fusion = s32[33600]{0:T(1024)S(1)} fusion(s32[8192]{0:T(1024)S(1)} %bitcast.108, s32[8192]{0:T(1024)S(1)} %iota.84, s32[]{:T(128)} %constant.166.clone.1), kind=kCustom, calls=%fused_computation.24 | custom fusion | bytes 134404 | tf_op jit(solution)/shard_map/scatter | solution.py:185
  45.7 1.8 rev.3
  50.2 4.3 all-to-all-start
  54.5 6.3 fusion.35
  64.3 1.9 fusion.26
  66.2 2.4 pad_add_fusion.5.ids
  68.6 34.3 %lend.1 = (bf16[3,2048,1408]{2,1,0:T(8,128)(2,1)}, bf16[3,2048,1408]{2,1,0:T(8,128)(2,1)}, bf16[3,1408,2048]{2,1,0:T(8,128)(2,1)}) custom-call(s32[3]{0:T(128)} %pad_add_fusion.5.ids, bf16[15,2048,1408]{2,1,0:T(8,128)(2,1)} %refs_2_.5, bf16[15,2048,1408]{2,1,0:T(8,128)(2,1)} %refs_3_.3, bf16[15,1408,2048]{2,1,0:T(8,128)(2,1)} %w2.3), custom_call_target="tpu_custom_call" | custom-call | flops 1000000000 | bytes 103809024 | tf_op jit(solution)/shard_map/lend/pallas_call | solution.py:207
  108.2 31.9 %fusion.42 = f32[2048,2816]{1,0:T(8,128)} fusion(bf16[2048,2048]{1,0:T(8,128)(2,1)} %param.11, bf16[2048,2816]{1,0:T(8,128)(2,1)} %param.16), kind=kOutput, calls=%fused_computation.146 | convolution fusion | flops 23622320128 | bytes 42991616 | tf_op jit(solution)/shard_map/dot_general | solution.py:312
  141.9 34.4 %multiply_convert_fusion.clone.4 = bf16[2048,2816]{1,0:T(8,128)(2,1)} fusion(f32[2048,2816]{1,0:T(8,128)} %fusion.42, bf16[2048,2048]{1,0:T(8,128)(2,1)} %param.11, bf16[2048,2816]{1,0:T(8,128)(2,1)} %param.17), kind=kOutput, calls=%fused_computation.2.clone.clone.clone.1 | convolution fusion | flops 23656923136 | bytes 54525952 | tf_op jit(solution)/shard_map/dot_general | solution.py:313
  176.3 32.3 %fusion.2 = f32[2048,2048]{1,0:T(8,128)} fusion(bf16[2816,2048]{1,0:T(8,128)(2,1)} %param.18, bf16[2048,2816]{1,0:T(8,128)(2,1)} %multiply_convert_fusion.clone.4), kind=kOutput, calls=%fused_computation.9 | convolution fusion | flops 23622320128 | bytes 39845888 | tf_op jit(solution)/shard_map/dot_general | solution.py:315
  213.5 2.0 fusion.29
  228.7 1.8 compare_not_fusion
  243.4 18.6 %fusion.43 = f32[1024,2816]{1,0:T(8,128)} fusion(bf16[1024,2048]{1,0:T(8,128)(2,1)} %collective-permute-done, bf16[2048,2816]{1,0:T(8,128)(2,1)} %param.16), kind=kOutput, calls=%fused_computation.147 | convolution fusion | flops 11811160064 | bytes 27262976 | tf_op jit(solution)/shard_map/dot_general | solution.py:312
  262.1 36.3 %fusion.3 = f32[1024,2048]{1,0:T(8,128)} fusion(bf16[2816,2048]{1,0:T(8,128)(2,1)} %param.18, f32[1024,2816]{1,0:T(8,128)} %fusion.43, bf16[1024,2048]{1,0:T(8,128)(2,1)} %collective-permute-done, bf16[2048,2816]{1,0:T(8,128)(2,1)} %param.17), kind=kOutput, calls=%fused_computation.10 | convolution fusion | flops 23639621632 | bytes 47185920 | tf_op jit(solution)/shard_map/dot_general | solution.py:315
  298.9 99.0 %expert_up.2.u_ref = bf16[20992,1408]{1,0:T(8,128)(2,1)} custom-call(s32[82]{0:T(128)} %broadcast_minimum_fusion.1.tile_exp, s32[83]{0:T(128)} %pad_add_fusion.3.tile_row, s32[54]{0:T(128)} %reshape.317.offs, s32[36]{0:T(128)} %pad_add_fusion.4.groups, s32[20160]{0:T(1024)} %reshape.319.owner, bf16[2048,16,128]{2,1,0:T(8,128)(2,1)} %collective-permute-done.3.refs_0_, ...), custom_call_target="tpu_custom_call" | custom-call | flops 94489280512 | bytes 173015040 | tf_op jit(solution)/shard_map/expert_up/pallas_call | solution.py:265
  397.9 81.6 %expert_down.2 = (f32[1024,2048]{1,0:T(8,128)}, f32[1024,2048]{1,0:T(8,128)}, f32[1024,2048]{1,0:T(8,128)}, f32[1024,2048]{1,0:T(8,128)}) custom-call(s32[82]{0:T(128)} %broadcast_minimum_fusion.1.tile_exp, s32[83]{0:T(128)} %pad_add_fusion.3.tile_row, s32[54]{0:T(128)} %reshape.317.offs, s32[36]{0:T(128)} %pad_add_fusion.4.groups, s32[20160]{0:T(1024)} %reshape.319.owner, ...), custom_call_target="tpu_custom_call" | custom-call | flops 47244640256 | bytes 86507520 | tf_op jit(solution)/shard_map/expert_down/pallas_call | solution.py:286
  479.5 13.0 %collective-permute-start.13 = (f32[1024,2048]{1,0:T(8,128)}, f32[1024,2048]{1,0:T(8,128)}, u32[]{:S(2)}, u32[]{:S(2)}) collective-permute-start(f32[1024,2048]{1,0:T(8,128)} %get-tuple-element.56), channel_id=1, source_target_pairs={{0,1},{1,0},{2,3},{3,2},{4,5},{5,4},{6,7},{7,6}} | collective-permute-start | bytes 25165832 | tf_op jit(solution)/shard_map/ppermute | solution.py:324
  492.5 18.7 %fusion.44 = f32[1024,2816]{1,0:T(8,128)} fusion(bf16[1024,2048]{1,0:T(8,128)(2,1)} %collective-permute-done.2, bf16[2048,2816]{1,0:T(8,128)(2,1)} %param.16), kind=kOutput, calls=%fused_computation.148 | convolution fusion | flops 11811160064 | bytes 27262976 | tf_op jit(solution)/shard_map/dot_general | solution.py:312
  511.2 36.2 %fusion.4 = f32[1024,2048]{1,0:T(8,128)} fusion(bf16[2816,2048]{1,0:T(8,128)(2,1)} %param.18, f32[1024,2816]{1,0:T(8,128)} %fusion.44, bf16[1024,2048]{1,0:T(8,128)(2,1)} %collective-permute-done.2, bf16[2048,2816]{1,0:T(8,128)(2,1)} %param.17), kind=kOutput, calls=%fused_computation.11 | convolution fusion | flops 23639621632 | bytes 47185920 | tf_op jit(solution)/shard_map/dot_general | solution.py:315
  547.4 99.1 %expert_up.3.u_ref = bf16[20992,1408]{1,0:T(8,128)(2,1)} custom-call(s32[82]{0:T(128)} %broadcast_minimum_fusion.tile_exp, s32[83]{0:T(128)} %pad_add_fusion.6.tile_row, s32[54]{0:T(128)} %reshape.323.offs, s32[36]{0:T(128)} %pad_add_fusion.7.groups, s32[20160]{0:T(1024)} %reshape.325.owner, bf16[2048,16,128]{2,1,0:T(8,128)(2,1)} %bitcast.104, ...), custom_call_target="tpu_custom_call" | custom-call | flops 94489280512 | bytes 173015040 | tf_op jit(solution)/shard_map/expert_up/pallas_call | solution.py:265
  646.6 81.0 %expert_down.3 = (f32[2048,2048]{1,0:T(8,128)}, f32[2048,2048]{1,0:T(8,128)}) custom-call(s32[82]{0:T(128)} %broadcast_minimum_fusion.tile_exp, s32[83]{0:T(128)} %pad_add_fusion.6.tile_row, s32[54]{0:T(128)} %reshape.323.offs, s32[36]{0:T(128)} %pad_add_fusion.7.groups, s32[20160]{0:T(1024)} %reshape.325.owner, f32[16416]{0:T(1024)} %concatenate.57.gates, ...), custom_call_target="tpu_custom_call" | custom-call | flops 47244640256 | bytes 86507520 | tf_op jit(solution)/shard_map/expert_down/pallas_call | solution.py:286
  727.6 14.1 %collective-permute-start.10 = (f32[2048,2048]{1,0:T(8,128)}, f32[2048,2048]{1,0:T(8,128)}, u32[]{:S(2)}, u32[]{:S(2)}) collective-permute-start(f32[2048,2048]{1,0:T(8,128)} %get-tuple-element.52), channel_id=1, source_target_pairs={{0,1},{1,0},{2,3},{3,2},{4,5},{5,4},{6,7},{7,6}} | collective-permute-start | bytes 50331656 | tf_op jit(solution)/shard_map/ppermute | solution.py:331
  743.7 11.9 %add.288 = f32[1024,2048]{1,0:T(8,128)} add(f32[1024,2048]{1,0:T(8,128)} %get-tuple-element.55, f32[1024,2048]{1,0:T(8,128)} %collective-permute-done.13) | non-fusion elementwise | flops 2097152 | bytes 25165824 | tf_op jit(solution)/shard_map/add | solution.py:325
  755.6 42.9 %collective-permute-start.14 = (f32[1024,2048]{1,0:T(8,128)}, f32[1024,2048]{1,0:T(8,128)}, u32[]{:S(2)}, u32[]{:S(2)}) collective-permute-start(f32[1024,2048]{1,0:T(8,128)} %add.288), channel_id=1, source_target_pairs={{0,2},{1,3},{2,0},{3,1},{4,6},{5,7},{6,4},{7,5}} | collective-permute-start | bytes 25165832 | tf_op jit(solution)/shard_map/ppermute | solution.py:328
  798.5 12.0 %add.287 = f32[1024,2048]{1,0:T(8,128)} add(f32[1024,2048]{1,0:T(8,128)} %get-tuple-element.53, f32[1024,2048]{1,0:T(8,128)} %collective-permute-done.11) | non-fusion elementwise | flops 2097152 | bytes 25165824 | tf_op jit(solution)/shard_map/add | solution.py:325
  810.5 114.8 %collective-permute-done.1 = f32[1024,2048]{1,0:T(8,128)} collective-permute-done((f32[1024,2048]{1,0:T(8,128)}, f32[1024,2048]{1,0:T(8,128)}, u32[]{:S(2)}, u32[]{:S(2)}) %collective-permute-start.1) | collective-permute-done | bytes 8388640 | tf_op jit(solution)/shard_map/ppermute | solution.py:329
  925.3 178.9 %collective-permute-done.8 = f32[1024,2048]{1,0:T(8,128)} collective-permute-done((f32[1024,2048]{1,0:T(8,128)}, f32[1024,2048]{1,0:T(8,128)}, u32[]{:S(2)}, u32[]{:S(2)}) %collective-permute-start.8) | collective-permute-done | bytes 8388640 | tf_op jit(solution)/shard_map/ppermute | solution.py:329
  1104.2 26.4 %fusion = f32[2048,2048]{1,0:T(8,128)} fusion(f32[2048,2048]{1,0:T(8,128)} %get-tuple-element.51, f32[1024,2048]{1,0:T(8,128)} %collective-permute-done.8, f32[1024,2048]{1,0:T(8,128)} %collective-permute-done.1, f32[2048,2048]{1,0:T(8,128)} %fusion.2, bf16[2048,2048]{1,0:T(8,128)(2,1)} %param.11), kind=kLoop, calls=%fused_computation.4 | loop fusion | flops 20971520 | bytes 75497472 | tf_op jit(solution)/shard_map/add | solution.py:332
  1130.6 27.9 %collective-permute-done.12 = f32[1024,2048]{1,0:T(8,128)S(1)} collective-permute-done((f32[1024,2048]{1,0:T(8,128)}, f32[1024,2048]{1,0:T(8,128)S(1)}, u32[]{:S(2)}, u32[]{:S(2)}) %collective-permute-start.12) | collective-permute-done | bytes 8388640 | tf_op jit(solution)/shard_map/ppermute | solution.py:328
  1158.5 18.1 %fusion.1 = bf16[2048,2048]{1,0:T(8,128)(2,1)} fusion(f32[1024,2048]{1,0:T(8,128)} %collective-permute-done.14, f32[1024,2048]{1,0:T(8,128)S(1)} %collective-permute-done.12, f32[2048,2048]{1,0:T(8,128)} %fusion, f32[2048,2048]{1,0:T(8,128)} %collective-permute-done.10), kind=kLoop, calls=%fused_computation.6 | loop fusion | flops 16777216 | bytes 58720256 | tf_op jit(solution)/shard_map/convert_element_type | solution.py:333
  (125 shorter events, 30.4 us)
Async XLA Ops:
  0.0 13.3 %copy-start.3 = (s32[1,60]{1,0:T(1,128)S(1)}, s32[1,60]{1,0:T(1,128)}, u32[]{:S(2)}) copy-start(s32[1,60]{1,0:T(1,128)} %param.15) | copy-start | bytes 724
  0.0 13.4 %copy-start = (s32[2048,4]{0,1:T(4,128)S(1)}, s32[2048,4]{0,1:T(4,128)}, u32[]{:S(2)}) copy-start(s32[2048,4]{0,1:T(4,128)} %param.12) | copy-start | bytes 98308
  0.0 13.4 %copy-start.1 = (s32[2048,4]{0,1:T(4,128)S(1)}, s32[2048,4]{0,1:T(4,128)}, u32[]{:S(2)}) copy-start(s32[2048,4]{0,1:T(4,128)} %param.14) | copy-start | bytes 98308
  0.0 47.7 %copy-start.2 = (f32[2048,4]{0,1:T(4,128)S(1)}, f32[2048,4]{0,1:T(4,128)}, u32[]{:S(2)}) copy-start(f32[2048,4]{0,1:T(4,128)} %param.13) | copy-start | bytes 98308
  10.0 233.1 %collective-permute-start.3 = (bf16[2048,16,128]{2,1,0:T(8,128)(2,1)}, bf16[2048,16,128]{2,1,0:T(8,128)(2,1)}, u32[]{:S(2)}, u32[]{:S(2)}) collective-permute-start(bf16[2048,16,128]{2,1,0:T(8,128)(2,1)} %bitcast.102), channel_id=1, source_target_pairs={{0,2},{1,3},{2,0},{3,1},{4,6},{5,7},{6,4},{7,5}} | collective-permute-start | bytes 25165832 | tf_op jit(solution)/shard_map/ppermute | solution.py:177
  13.3 534.1 %collective-permute-start.9 = (bf16[2048,16,128]{2,1,0:T(8,128)(2,1)}, bf16[2048,16,128]{2,1,0:T(8,128)(2,1)}, u32[]{:S(2)}, u32[]{:S(2)}) collective-permute-start(bf16[2048,16,128]{2,1,0:T(8,128)(2,1)} %bitcast.103), channel_id=1, source_target_pairs={{0,1},{1,0},{2,3},{3,2},{4,5},{5,4},{6,7},{7,6}} | collective-permute-start | bytes 25165832 | tf_op jit(solution)/shard_map/ppermute | solution.py:179
  50.2 158.4 %all-to-all-start = ((f32[4,1,24992]{2,1,0:T(1,128)}), f32[4,1,24992]{2,1,0:T(1,128)}, u32[]{:S(2)}, u32[]{:S(2)}) async-start(f32[4,1,24992]{2,1,0:T(1,128)} %all_to_all.8), calls=%async_computation | async-start | bytes 802816 | tf_op jit(solution)/shard_map/all_to_all | solution.py:190
  60.8 182.1 %collective-permute-start = (bf16[1024,2048]{1,0:T(8,128)(2,1)}, bf16[1024,2048]{1,0:T(8,128)(2,1)}, u32[]{:S(2)}, u32[]{:S(2)}) collective-permute-start(bf16[1024,2048]{1,0:T(8,128)(2,1)} %get-tuple-element.75), channel_id=1, source_target_pairs={{0,4},{4,0},{1,5},{5,1},{2,6},{6,2},{3,7},{7,3}} | collective-permute-start | bytes 12582920 | tf_op jit(solution)/shard_map/ppermute | solution.py:178
  102.9 196.0 %collective-permute-start.5 = (bf16[3,2048,1408]{2,1,0:T(8,128)(2,1)}, bf16[3,2048,1408]{2,1,0:T(8,128)(2,1)}, u32[]{:S(2)}, u32[]{:S(2)}) collective-permute-start(bf16[3,2048,1408]{2,1,0:T(8,128)(2,1)} %get-tuple-element.41), channel_id=1, source_target_pairs={{0,1},{1,0},{2,3},{3,2},{4,5},{5,4},{6,7},{7,6}} | collective-permute-start | bytes 51904520 | tf_op jit(solution)/shard_map/ppermute | solution.py:215
  103.1 195.7 %collective-permute-start.6 = (bf16[3,2048,1408]{2,1,0:T(8,128)(2,1)}, bf16[3,2048,1408]{2,1,0:T(8,128)(2,1)}, u32[]{:S(2)}, u32[]{:S(2)}) collective-permute-start(bf16[3,2048,1408]{2,1,0:T(8,128)(2,1)} %get-tuple-element.42), channel_id=1, source_target_pairs={{0,1},{1,0},{2,3},{3,2},{4,5},{5,4},{6,7},{7,6}} | collective-permute-start | bytes 51904520 | tf_op jit(solution)/shard_map/ppermute | solution.py:215
  176.3 32.3 %copy-start.4 = (s32[4]{0:T(128)S(1)}, s32[4]{0:T(128)}, u32[]{:S(2)}) copy-start(s32[4]{0:T(128)} %fusion.30) | copy-start | bytes 52
  176.3 34.2 %copy-start.5 = (pred[4]{0:T(512)(128)(4,1)S(1)}, pred[4]{0:T(512)(128)(4,1)}, u32[]{:S(2)}) copy-start(pred[4]{0:T(512)(128)(4,1)} %compare_and_fusion) | copy-start | bytes 16
  242.9 155.0 %collective-permute-start.7 = (bf16[3,1408,2048]{2,1,0:T(8,128)(2,1)}, bf16[3,1408,2048]{2,1,0:T(8,128)(2,1)}, u32[]{:S(2)}, u32[]{:S(2)}) collective-permute-start(bf16[3,1408,2048]{2,1,0:T(8,128)(2,1)} %get-tuple-element.43), channel_id=1, source_target_pairs={{0,1},{1,0},{2,3},{3,2},{4,5},{5,4},{6,7},{7,6}} | collective-permute-start | bytes 51904520 | tf_op jit(solution)/shard_map/ppermute | solution.py:215
  243.1 55.2 %collective-permute-start.4 = (bf16[2048,16,128]{2,1,0:T(8,128)(2,1)}, bf16[2048,16,128]{2,1,0:T(8,128)(2,1)}, u32[]{:S(2)}, u32[]{:S(2)}) collective-permute-start(bf16[2048,16,128]{2,1,0:T(8,128)(2,1)} %collective-permute-done.3.refs_0_), channel_id=1, source_target_pairs={{0,1},{1,0},{2,3},{3,2},{4,5},{5,4},{6,7},{7,6}} | collective-permute-start | bytes 25165832 | tf_op jit(solution)/shard_map/ppermute | solution.py:180
  298.4 181.1 %collective-permute-start.2 = (bf16[1024,2048]{1,0:T(8,128)(2,1)}, bf16[1024,2048]{1,0:T(8,128)(2,1)}, u32[]{:S(2)}, u32[]{:S(2)}) collective-permute-start(bf16[1024,2048]{1,0:T(8,128)(2,1)} %get-tuple-element.76), channel_id=1, source_target_pairs={{0,4},{4,0},{1,5},{5,1},{2,6},{6,2},{3,7},{7,3}} | collective-permute-start | bytes 12582920 | tf_op jit(solution)/shard_map/ppermute | solution.py:178
  479.5 264.2 %collective-permute-start.13 = (f32[1024,2048]{1,0:T(8,128)}, f32[1024,2048]{1,0:T(8,128)}, u32[]{:S(2)}, u32[]{:S(2)}) collective-permute-start(f32[1024,2048]{1,0:T(8,128)} %get-tuple-element.56), channel_id=1, source_target_pairs={{0,1},{1,0},{2,3},{3,2},{4,5},{5,4},{6,7},{7,6}} | collective-permute-start | bytes 25165832 | tf_op jit(solution)/shard_map/ppermute | solution.py:324
  492.4 306.0 %collective-permute-start.11 = (f32[1024,2048]{1,0:T(8,128)}, f32[1024,2048]{1,0:T(8,128)}, u32[]{:S(2)}, u32[]{:S(2)}) collective-permute-start(f32[1024,2048]{1,0:T(8,128)} %get-tuple-element.54), channel_id=1, source_target_pairs={{0,1},{1,0},{2,3},{3,2},{4,5},{5,4},{6,7},{7,6}} | collective-permute-start | bytes 25165832 | tf_op jit(solution)/shard_map/ppermute | solution.py:324
  727.6 430.9 %collective-permute-start.10 = (f32[2048,2048]{1,0:T(8,128)}, f32[2048,2048]{1,0:T(8,128)}, u32[]{:S(2)}, u32[]{:S(2)}) collective-permute-start(f32[2048,2048]{1,0:T(8,128)} %get-tuple-element.52), channel_id=1, source_target_pairs={{0,1},{1,0},{2,3},{3,2},{4,5},{5,4},{6,7},{7,6}} | collective-permute-start | bytes 50331656 | tf_op jit(solution)/shard_map/ppermute | solution.py:331
  741.7 183.6 %collective-permute-start.1 = (f32[1024,2048]{1,0:T(8,128)}, f32[1024,2048]{1,0:T(8,128)}, u32[]{:S(2)}, u32[]{:S(2)}) collective-permute-start(f32[1024,2048]{1,0:T(8,128)} %fusion.3), channel_id=1, source_target_pairs={{0,4},{4,0},{1,5},{5,1},{2,6},{6,2},{3,7},{7,3}} | collective-permute-start | bytes 25165832 | tf_op jit(solution)/shard_map/ppermute | solution.py:329
  743.4 360.7 %collective-permute-start.8 = (f32[1024,2048]{1,0:T(8,128)}, f32[1024,2048]{1,0:T(8,128)}, u32[]{:S(2)}, u32[]{:S(2)}) collective-permute-start(f32[1024,2048]{1,0:T(8,128)} %fusion.4), channel_id=1, source_target_pairs={{0,4},{4,0},{1,5},{5,1},{2,6},{6,2},{3,7},{7,3}} | collective-permute-start | bytes 25165832 | tf_op jit(solution)/shard_map/ppermute | solution.py:329
  755.6 375.0 %collective-permute-start.14 = (f32[1024,2048]{1,0:T(8,128)}, f32[1024,2048]{1,0:T(8,128)}, u32[]{:S(2)}, u32[]{:S(2)}) collective-permute-start(f32[1024,2048]{1,0:T(8,128)} %add.288), channel_id=1, source_target_pairs={{0,2},{1,3},{2,0},{3,1},{4,6},{5,7},{6,4},{7,5}} | collective-permute-start | bytes 25165832 | tf_op jit(solution)/shard_map/ppermute | solution.py:328
  810.5 348.1 %collective-permute-start.12 = (f32[1024,2048]{1,0:T(8,128)}, f32[1024,2048]{1,0:T(8,128)S(1)}, u32[]{:S(2)}, u32[]{:S(2)}) collective-permute-start(f32[1024,2048]{1,0:T(8,128)} %add.287), channel_id=1, source_target_pairs={{0,2},{1,3},{2,0},{3,1},{4,6},{5,7},{6,4},{7,5}} | collective-permute-start | bytes 25165832 | tf_op jit(solution)/shard_map/ppermute | solution.py:328
